TPU v7x, 32 devices: a whole 2x2x4 slice. The times are simulated.
32 devices in a mesh: groups: 2 (over y), batch: 8 (over z, x), mp: 2 (over core).
Axes of the slice: x: 2, y: 2, z: 4, core: 2. Of those that a mesh axis runs over, the one named last changes fastest.
Arguments:
- hidden: bfloat16 [32, 1280], P(('groups', 'batch')), parts along dimension 0, may hold values from -6 to 6
- token_qkv: bfloat16 [3, 32, 1280], P(None, ('groups', 'batch'), 'mp'), parts along dimension 1, may hold values from -6 to 6
- self_cache: bfloat16 [2, 32, 128, 1280], P(None, ('groups', 'batch'), None, 'mp'), parts along dimension 1, may hold values from -6 to 6
- cross_kv: bfloat16 [2, 32, 64, 1280], P(None, ('groups', 'batch'), None, 'mp'), parts along dimension 1, may hold values from -6 to 6
- cache_len: int32 [32], P(('groups', 'batch')), parts along dimension 0, may hold values from 1 to 127
- finished: int32 [32], P(('groups', 'batch')), parts along dimension 0, may hold values 0 or 1
- new_slot: int32 [32], P(('groups', 'batch')), parts along dimension 0, may hold values from 0 to 15, as said below
- out_proj: bfloat16 [1280, 1280], P('mp'), may hold values from -0.15625 to 0.15625
- ln_gain: float32 [1280], replicated, may hold values from 0.5 to 1.5
- ln_bias: float32 [1280], replicated, may hold values from -3 to 3
- query_proj: bfloat16 [1280, 1280], P(None, 'mp'), may hold values from -3 to 3
Outputs:
- moved_cache: bfloat16 [2, 32, 128, 1280], P(None, ('groups', 'batch'), None, 'mp'), parts along dimension 1
- moved_out: bfloat16 [32, 1280], P(('groups', 'batch'), 'mp'), parts along dimension 0
There are 2 independent parts, one for each index of `groups`. A program takes and returns all parts, laid end to end along the dimension named above; an argument that names none is the same for every part. Nothing has to cross between parts.
Inputs may be any that keep to these rules, and one draw needn't show every extreme that they name: A permutation of the spans' slots. Span c's new owner new_slot[c] // 2 lies within 3 devices of its present one c // 2, counting the device order as a loop; of one device's spans at most one moves by any given signed distance.
All inputs are finite; a program needn't handle non-finite values. No bound on the sum of `finished` on one device may be relied on, other than what follows from the above.
Results may differ from a plain program's by a relative error of at most 0.015.
Values may be sent and summed in bfloat16 or wider, within the bound.
A program may use at most 64 MiB of HBM per device.

v0:
```python
import jax
import jax.numpy as jnp
from jax import lax
from jax.sharding import PartitionSpec as P

HEAD_DIM = 64
REACH = 3


def passed_along(block, axis, distance):
    devices = range(lax.axis_size(axis))
    route = [((i - distance) % len(devices), i) for i in devices]
    return lax.ppermute(block, axis, route)


def body(
    hidden,
    token_qkv,
    self_cache,
    cross_kv,
    cache_len,
    finished,
    new_slot,
    out_proj,
    ln_gain,
    ln_bias,
    query_proj,
):
    spans = hidden.shape[0]
    slots = self_cache.shape[2]
    local_width = self_cache.shape[3]
    frames = cross_kv.shape[2]
    head_count = local_width // HEAD_DIM
    factor = HEAD_DIM ** (-0.5)
    new_query = token_qkv[0].reshape(spans, head_count, HEAD_DIM)
    new_key = token_qkv[1].reshape(spans, head_count, HEAD_DIM)
    new_value = token_qkv[2].reshape(spans, head_count, HEAD_DIM)
    cache_keys = self_cache[0].reshape(spans, slots, head_count, HEAD_DIM)
    cache_values = self_cache[1].reshape(spans, slots, head_count, HEAD_DIM)
    scores = (
        jnp.einsum("chd,cthd->cht", new_query, cache_keys, preferred_element_type=jnp.float32)
        * factor
    )
    position = jnp.arange(slots, dtype=jnp.int32)
    usable = position[None, None, :] < cache_len[:, None, None]
    scores = jnp.where(usable, scores, -1e30)
    own_score = (
        jnp.sum(new_query.astype(jnp.float32) * new_key.astype(jnp.float32), axis=-1) * factor
    )
    highest = jnp.maximum(jnp.max(scores, axis=-1), own_score)
    cache_weight = jnp.where(usable, jnp.exp(scores - highest[..., None]), 0.0)
    own_weight = jnp.exp(own_score - highest)
    total = jnp.sum(cache_weight, axis=-1) + own_weight
    cache_weight = (cache_weight / total[..., None]).astype(jnp.bfloat16)
    own_weight = (own_weight / total).astype(jnp.bfloat16)
    context = jnp.einsum(
        "cht,cthd->chd", cache_weight, cache_values, preferred_element_type=jnp.float32
    )
    context = context + own_weight.astype(jnp.float32)[..., None] * new_value.astype(jnp.float32)
    context = context.astype(jnp.bfloat16).reshape(spans, local_width)
    partial_proj = jnp.dot(context, out_proj, preferred_element_type=jnp.float32)
    resid = hidden.astype(jnp.float32) + lax.psum(partial_proj, "mp")
    centre = jnp.mean(resid, axis=-1, keepdims=True)
    spread = jnp.mean((resid - centre) ** 2, axis=-1, keepdims=True)
    normed = ((resid - centre) * lax.rsqrt(spread + 1e-05) * ln_gain + ln_bias).astype(jnp.bfloat16)
    cross_query = jnp.dot(normed, query_proj, preferred_element_type=jnp.float32).astype(
        jnp.bfloat16
    )
    cross_query = cross_query.reshape(spans, head_count, HEAD_DIM)
    cross_keys = cross_kv[0].reshape(spans, frames, head_count, HEAD_DIM)
    cross_values = cross_kv[1].reshape(spans, frames, head_count, HEAD_DIM)
    cross_scores = (
        jnp.einsum("chd,cthd->cht", cross_query, cross_keys, preferred_element_type=jnp.float32)
        * factor
    )
    cross_high = jnp.max(cross_scores, axis=-1, keepdims=True)
    cross_exp = jnp.exp(cross_scores - cross_high)
    cross_weight = (cross_exp / jnp.sum(cross_exp, axis=-1, keepdims=True)).astype(jnp.bfloat16)
    cross_context = jnp.einsum(
        "cht,cthd->chd", cross_weight, cross_values, preferred_element_type=jnp.float32
    )
    cross_context = cross_context.reshape(spans, local_width)
    alive = finished == 0
    decoded = jnp.where(alive[:, None], cross_context, 0.0).astype(jnp.bfloat16)
    slot_pos = position[None, :, None]
    length = cache_len[:, None, None]

    def extend(older, fresh):
        grown = jnp.where(
            slot_pos < length,
            older,
            jnp.where(slot_pos == length, fresh[:, None, :], jnp.zeros_like(older)),
        )
        return jnp.where(alive[:, None, None], grown, jnp.zeros_like(older))

    updated = jnp.stack([extend(self_cache[0], token_qkv[1]), extend(self_cache[1], token_qkv[2])])
    device_index = lax.axis_index("batch")
    device_count = lax.axis_size("batch")
    dest_device = new_slot // spans
    dest_local = new_slot % spans
    half_count = device_count // 2
    offset = (dest_device - device_index + half_count) % device_count - half_count
    placing = dest_local[:, None] == jnp.arange(spans, dtype=jnp.int32)[None, :]
    select = ((offset == 0)[:, None] & placing).astype(jnp.bfloat16)
    cache_part = jnp.einsum("jl,ajtd->altd", select, updated, preferred_element_type=jnp.float32)
    out_part = jnp.einsum("jl,jd->ld", select, decoded, preferred_element_type=jnp.float32)
    cache_total = cache_part
    out_total = out_part
    distances = [shift_by for shift_by in range(-REACH, REACH + 1) if shift_by != 0]
    placing_weights = placing.astype(jnp.bfloat16)
    for distance in distances:
        picked = (offset == distance).astype(jnp.bfloat16)
        payload = jnp.einsum(
            "j,ajtd->atd", picked, updated, preferred_element_type=jnp.float32
        ).astype(jnp.bfloat16)
        out_row = jnp.einsum("j,jd->d", picked, decoded, preferred_element_type=jnp.float32).astype(
            jnp.bfloat16
        )
        marker = jnp.einsum(
            "j,jl->l", picked, placing_weights, preferred_element_type=jnp.float32
        ).astype(jnp.bfloat16)
        marker_row = jnp.pad(marker, (0, local_width - spans))
        parcel = jnp.concatenate(
            [payload.reshape(2 * slots, local_width), out_row[None, :], marker_row[None, :]], 0
        )
        arrived = passed_along(parcel, "batch", distance)
        got_cache = arrived[: 2 * slots].reshape(2, slots, local_width)
        got_out = arrived[2 * slots]
        got_marker = arrived[2 * slots + 1, :spans]
        cache_total = cache_total + jnp.einsum(
            "l,atd->altd", got_marker, got_cache, preferred_element_type=jnp.float32
        )
        out_total = out_total + jnp.einsum(
            "l,d->ld", got_marker, got_out, preferred_element_type=jnp.float32
        )
    return (cache_total.astype(jnp.bfloat16), out_total.astype(jnp.bfloat16))


def solution(mesh):
    placed = (
        P(("groups", "batch"), None),
        P(None, ("groups", "batch"), "mp"),
        P(None, ("groups", "batch"), None, "mp"),
        P(None, ("groups", "batch"), None, "mp"),
        P(("groups", "batch")),
        P(("groups", "batch")),
        P(("groups", "batch")),
        P("mp", None),
        P(),
        P(),
        P(None, "mp"),
    )
    return jax.shard_map(
        body,
        mesh=mesh,
        in_specs=placed,
        out_specs=(P(None, ("groups", "batch"), None, "mp"), P(("groups", "batch"), "mp")),
        check_vma=False,
    )
```

profile of v0, /device:TPU:0, one launch (start us, length us, event | category | flops | bytes accessed | tf_op | source)
XLA Modules:
  0.0 73.9 jit_solution(7595137023181034762)
XLA Ops:
  0.7 0.9 %slice_bitcast_fusion.1 = (bf16[2,640]{1,0:T(2,128)(2,1)S(1)}, f32[1,2,640]{2,1,0:T(2,128)S(1)}, f32[1,2,640]{2,1,0:T(2,128)S(1)}, bf16[1,2,640]{2,1,0:T(2,128)(2,1)S(1)}, bf16[2,640]{1,0:T(2,128)(2,1)S(1)}) fusion(bf16[3,2,640]{2,1,0:T(2,128)(2,1)} %param.12), kind=kLoop, calls=%fused_computation.120 | loop fusion | flops 2560 | bytes 25600 | tf_op jit(solution)/shard_map/jit(_where)/broadcast_in_dim | solution.py:92
  3.0 0.7 broadcast_compare_fusion.6
  4.0 0.7 iota_compare_fusion
  4.8 1.0 %fusion.109 = (bf16[1,2,64,640]{3,2,1,0:T(8,128)(2,1)S(1)}, bf16[1,2,64,640]{3,2,1,0:T(8,128)(2,1)S(1)}) fusion(bf16[2,2,64,640]{3,2,1,0:T(8,128)(2,1)} %param.14), kind=kLoop, calls=%fused_computation.189 | loop fusion | bytes 655360 | tf_op jit(solution)/shard_map/slice | solution.py:70
  5.8 0.9 %copy.79 = bf16[1,2,64,640]{2,3,1,0:T(8,128)(2,1)} copy(bf16[1,2,64,640]{3,2,1,0:T(8,128)(2,1)S(1)} %get-tuple-element.18) | data formatting | bytes 327680
  9.3 3.6 %psum.7 = f32[2,1280]{1,0:T(2,128)S(1)} all-reduce(f32[2,1280]{1,0:T(2,128)S(1)} %fusion.111), channel_id=1, replica_groups=mesh['groups'=2,'batch'=8,'mp'=2] {'mp'}, use_global_device_ids=true, to_apply=%region_3.4 | all-reduce | flops 2560 | bytes 20480 | tf_op jit(solution)/shard_map/psum | solution.py:62
  13.3 1.8 %convolution_convert_fusion = bf16[2,640]{1,0:T(2,128)(2,1)S(1)} fusion(bf16[1280,640]{1,0:T(8,128)(2,1)} %param.21, f32[2]{0:T(128)S(1)} %add_rsqrt_fusion, f32[2]{0:T(128)S(1)} %broadcast_multiply_fusion, f32[1280]{0:T(1024)S(1)} %copy-done.4, f32[1280]{0:T(1024)S(1)} %copy-done.5, f32[2,1280]{1,0:T(2,128)S(1)} %psum.7, bf16[2,1280]{1,0:T(2,128)(2,1)S(1)} %copy-done.3), kind=kOutput, calls=%fused_computation.8 | convolution fusion | flops 3296000 | bytes 1666576 | tf_op jit(solution)/shard_map/dot_general | solution.py:66
  16.2 1.4 %broadcast_select_fusion.5 = (bf16[1,2,128,640]{3,1,2,0:T(2,128)(2,1)S(1)}, bf16[1,2,128,640]{3,1,2,0:T(2,128)(2,1)S(1)}) fusion(pred[2]{0:T(512)(128)(4,1)S(1)} %broadcast_compare_fusion.7, pred[2,128]{0,1:T(8,128)(4,1)S(1)} %get-tuple-element.30, pred[2,128]{0,1:T(8,128)(4,1)S(1)} %get-tuple-element.29, bf16[1,2,128,640]{3,2,1,0:T(8,128)(2,1)S(1)} %get-tuple-element.16, ...), kind=kLoop, calls=%fused_computation.39 | loop fusion | flops 983040 | bytes 1316354 | tf_op jit(solution)/shard_map/jit(_where)/select_n | solution.py:94
  17.6 0.9 %pad_maximum_fusion = bf16[2,2,128,640]{3,1,2,0:T(2,128)(2,1)S(1)} fusion(bf16[1,2,128,640]{3,1,2,0:T(2,128)(2,1)S(1)} %get-tuple-element.21, bf16[1,2,128,640]{3,1,2,0:T(2,128)(2,1)S(1)} %get-tuple-element.20), kind=kLoop, calls=%fused_computation.27 | loop fusion | flops 327680 | bytes 1310720 | tf_op jit(solution)/shard_map/stack | solution.py:96
  18.6 0.8 %fusion.49 = bf16[1,2,128,640]{3,0,2,1:T(2,128)(2,1)S(1)} fusion(bf16[2,2,128,640]{3,1,2,0:T(2,128)(2,1)S(1)} %pad_maximum_fusion, s32[2]{0:T(128)S(1)} %get-tuple-element.13), kind=kOutput, calls=%fused_computation.105 | convolution fusion | flops 655362 | bytes 983048 | tf_op jit(solution)/shard_map/j,ajtd->atd/dot_general | solution.py:113
  19.5 3.7 %collective-permute-start.5 = (bf16[258,640]{1,0:T(8,128)(2,1)S(1)}, bf16[258,640]{1,0:T(8,128)(2,1)S(1)}, u32[]{:S(2)}, u32[]{:S(2)}) collective-permute-start(bf16[258,640]{1,0:T(8,128)(2,1)S(1)} %pad_maximum_fusion.6), channel_id=1, source_target_pairs={{10,0},{12,2},{14,4},{0,6},{2,8},{4,10},{6,12},{8,14},{11,1},{13,3... | collective-permute-start | bytes 990728 | tf_op jit(solution)/shard_map/ppermute | solution.py:13
  23.5 0.8 %fusion.51 = bf16[1,2,128,640]{3,0,2,1:T(2,128)(2,1)S(1)} fusion(bf16[2,2,128,640]{3,1,2,0:T(2,128)(2,1)S(1)} %pad_maximum_fusion, s32[2]{0:T(128)S(1)} %get-tuple-element.13), kind=kOutput, calls=%fused_computation.107 | convolution fusion | flops 655362 | bytes 983048 | tf_op jit(solution)/shard_map/j,ajtd->atd/dot_general | solution.py:113
  24.4 1.6 %collective-permute-start.4 = (bf16[258,640]{1,0:T(8,128)(2,1)S(1)}, bf16[258,640]{1,0:T(8,128)(2,1)S(1)}, u32[]{:S(2)}, u32[]{:S(2)}) collective-permute-start(bf16[258,640]{1,0:T(8,128)(2,1)S(1)} %pad_maximum_fusion.5), channel_id=1, source_target_pairs={{12,0},{14,2},{0,4},{2,6},{4,8},{6,10},{8,12},{10,14},{13,1},{15,3... | collective-permute-start | bytes 990728 | tf_op jit(solution)/shard_map/ppermute | solution.py:13
  26.3 0.8 %fusion.53 = bf16[1,2,128,640]{3,0,2,1:T(2,128)(2,1)S(1)} fusion(bf16[2,2,128,640]{3,1,2,0:T(2,128)(2,1)S(1)} %pad_maximum_fusion, s32[2]{0:T(128)S(1)} %get-tuple-element.13), kind=kOutput, calls=%fused_computation.109 | convolution fusion | flops 655362 | bytes 983048 | tf_op jit(solution)/shard_map/j,ajtd->atd/dot_general | solution.py:113
  27.3 1.6 %collective-permute-start.3 = (bf16[258,640]{1,0:T(8,128)(2,1)S(1)}, bf16[258,640]{1,0:T(8,128)(2,1)S(1)}, u32[]{:S(2)}, u32[]{:S(2)}) collective-permute-start(bf16[258,640]{1,0:T(8,128)(2,1)S(1)} %pad_maximum_fusion.4), channel_id=1, source_target_pairs={{14,0},{0,2},{2,4},{4,6},{6,8},{8,10},{10,12},{12,14},{15,1},{1,3}... | collective-permute-start | bytes 990728 | tf_op jit(solution)/shard_map/ppermute | solution.py:13
  29.1 0.8 %fusion.55 = bf16[1,2,128,640]{3,0,2,1:T(2,128)(2,1)S(1)} fusion(bf16[2,2,128,640]{3,1,2,0:T(2,128)(2,1)S(1)} %pad_maximum_fusion, s32[2]{0:T(128)S(1)} %get-tuple-element.13), kind=kOutput, calls=%fused_computation.111 | convolution fusion | flops 655362 | bytes 983048 | tf_op jit(solution)/shard_map/j,ajtd->atd/dot_general | solution.py:113
  30.1 3.2 %collective-permute-start.2 = (bf16[258,640]{1,0:T(8,128)(2,1)S(1)}, bf16[258,640]{1,0:T(8,128)(2,1)S(1)}, u32[]{:S(2)}, u32[]{:S(2)}) collective-permute-start(bf16[258,640]{1,0:T(8,128)(2,1)S(1)} %pad_maximum_fusion.3), channel_id=1, source_target_pairs={{2,0},{4,2},{6,4},{8,6},{10,8},{12,10},{14,12},{0,14},{3,1},{5,3},... | collective-permute-start | bytes 990728 | tf_op jit(solution)/shard_map/ppermute | solution.py:13
  33.6 0.8 %fusion.57 = bf16[1,2,128,640]{3,0,2,1:T(2,128)(2,1)S(1)} fusion(bf16[2,2,128,640]{3,1,2,0:T(2,128)(2,1)S(1)} %pad_maximum_fusion, s32[2]{0:T(128)S(1)} %get-tuple-element.13), kind=kOutput, calls=%fused_computation.113 | convolution fusion | flops 655362 | bytes 983048 | tf_op jit(solution)/shard_map/j,ajtd->atd/dot_general | solution.py:113
  35.4 0.8 %fusion.59 = bf16[1,2,128,640]{3,0,2,1:T(2,128)(2,1)S(1)} fusion(bf16[2,2,128,640]{3,1,2,0:T(2,128)(2,1)S(1)} %pad_maximum_fusion, s32[2]{0:T(128)S(1)} %get-tuple-element.13), kind=kOutput, calls=%fused_computation.115 | convolution fusion | flops 655362 | bytes 983048 | tf_op jit(solution)/shard_map/j,ajtd->atd/dot_general | solution.py:113
  36.3 18.5 %collective-permute-done.5 = bf16[258,640]{1,0:T(8,128)(2,1)S(1)} collective-permute-done((bf16[258,640]{1,0:T(8,128)(2,1)S(1)}, bf16[258,640]{1,0:T(8,128)(2,1)S(1)}, u32[]{:S(2)}, u32[]{:S(2)}) %collective-permute-start.5) | collective-permute-done | bytes 330272 | tf_op jit(solution)/shard_map/ppermute | solution.py:13
  55.5 13.4 %collective-permute-done = bf16[258,640]{1,0:T(8,128)(2,1)S(1)} collective-permute-done((bf16[258,640]{1,0:T(8,128)(2,1)S(1)}, bf16[258,640]{1,0:T(8,128)(2,1)S(1)}, u32[]{:S(2)}, u32[]{:S(2)}) %collective-permute-start) | collective-permute-done | bytes 330272 | tf_op jit(solution)/shard_map/ppermute | solution.py:13
  69.0 3.1 %fusion.13 = bf16[2,2,128,640]{3,1,2,0:T(2,128)(2,1)S(1)} fusion(f32[2]{0:T(128)S(1)} %fusion.70, f32[2,128,640]{2,1,0:T(8,128)S(1)} %convert.145, f32[2]{0:T(128)S(1)} %fusion.71, f32[2,128,640]{2,1,0:T(8,128)S(1)} %convert.144, f32[2]{0:T(128)S(1)} %fusion.72, f32[2,128,640]{2,1,0:T(8,128)S(1)} %convert.143, f32[2]{0:T(128)S(1)} %fusion.73, ...), kind=kOutput, calls=%fused_computation.40 | convolution fusion | flops 5570568 | bytes 5242938 | tf_op jit(solution)/shard_map/jl,ajtd->altd/dot_general | solution.py:105
  72.2 0.9 %copy.55 = bf16[2,2,128,640]{3,2,1,0:T(8,128)(2,1)} copy(bf16[2,2,128,640]{3,1,2,0:T(2,128)(2,1)S(1)} %fusion.13) | data formatting | bytes 1310720
  73.2 0.7 add_convert_fusion.3
  (121 shorter events, 9.0 us)
Async XLA Ops:
  0.6 8.3 %copy-start = (bf16[640,1280]{1,0:T(8,128)(2,1)S(1)}, bf16[640,1280]{1,0:T(8,128)(2,1)}, u32[]{:S(2)}) copy-start(bf16[640,1280]{1,0:T(8,128)(2,1)} %param.18) | copy-start | bytes 4915204
  0.6 6.3 %copy-start.1 = (bf16[2,2,128,640]{3,2,1,0:T(8,128)(2,1)S(1)}, bf16[2,2,128,640]{3,2,1,0:T(8,128)(2,1)}, u32[]{:S(2)}) copy-start(bf16[2,2,128,640]{3,2,1,0:T(8,128)(2,1)} %param.13) | copy-start | bytes 1966084
  8.2 4.7 %copy-start.3 = (bf16[2,1280]{1,0:T(2,128)(2,1)S(1)}, bf16[2,1280]{1,0:T(2,128)(2,1)}, u32[]{:S(2)}) copy-start(bf16[2,1280]{1,0:T(2,128)(2,1)} %param.11) | copy-start | bytes 15364
  8.2 5.1 %copy-start.4 = (f32[1280]{0:T(1024)S(1)}, f32[1280]{0:T(1024)}, u32[]{:S(2)}) copy-start(f32[1280]{0:T(1024)} %param.20) | copy-start | bytes 15364
  8.2 5.1 %copy-start.5 = (f32[1280]{0:T(1024)S(1)}, f32[1280]{0:T(1024)}, u32[]{:S(2)}) copy-start(f32[1280]{0:T(1024)} %param.19) | copy-start | bytes 15364
  9.0 6.2 %copy-start.2 = (bf16[1,2,64,640]{2,3,1,0:T(8,128)(2,1)S(1)}, bf16[1,2,64,640]{2,3,1,0:T(8,128)(2,1)}, u32[]{:S(2)}) copy-start(bf16[1,2,64,640]{2,3,1,0:T(8,128)(2,1)} %copy.79) | copy-start | bytes 491524
  19.5 35.3 %collective-permute-start.5 = (bf16[258,640]{1,0:T(8,128)(2,1)S(1)}, bf16[258,640]{1,0:T(8,128)(2,1)S(1)}, u32[]{:S(2)}, u32[]{:S(2)}) collective-permute-start(bf16[258,640]{1,0:T(8,128)(2,1)S(1)} %pad_maximum_fusion.6), channel_id=1, source_target_pairs={{10,0},{12,2},{14,4},{0,6},{2,8},{4,10},{6,12},{8,14},{11,1},{13,3... | collective-permute-start | bytes 990728 | tf_op jit(solution)/shard_map/ppermute | solution.py:13
  24.4 30.4 %collective-permute-start.4 = (bf16[258,640]{1,0:T(8,128)(2,1)S(1)}, bf16[258,640]{1,0:T(8,128)(2,1)S(1)}, u32[]{:S(2)}, u32[]{:S(2)}) collective-permute-start(bf16[258,640]{1,0:T(8,128)(2,1)S(1)} %pad_maximum_fusion.5), channel_id=1, source_target_pairs={{12,0},{14,2},{0,4},{2,6},{4,8},{6,10},{8,12},{10,14},{13,1},{15,3... | collective-permute-start | bytes 990728 | tf_op jit(solution)/shard_map/ppermute | solution.py:13
  27.3 27.7 %collective-permute-start.3 = (bf16[258,640]{1,0:T(8,128)(2,1)S(1)}, bf16[258,640]{1,0:T(8,128)(2,1)S(1)}, u32[]{:S(2)}, u32[]{:S(2)}) collective-permute-start(bf16[258,640]{1,0:T(8,128)(2,1)S(1)} %pad_maximum_fusion.4), channel_id=1, source_target_pairs={{14,0},{0,2},{2,4},{4,6},{6,8},{8,10},{10,12},{12,14},{15,1},{1,3}... | collective-permute-start | bytes 990728 | tf_op jit(solution)/shard_map/ppermute | solution.py:13
  30.1 25.0 %collective-permute-start.2 = (bf16[258,640]{1,0:T(8,128)(2,1)S(1)}, bf16[258,640]{1,0:T(8,128)(2,1)S(1)}, u32[]{:S(2)}, u32[]{:S(2)}) collective-permute-start(bf16[258,640]{1,0:T(8,128)(2,1)S(1)} %pad_maximum_fusion.3), channel_id=1, source_target_pairs={{2,0},{4,2},{6,4},{8,6},{10,8},{12,10},{14,12},{0,14},{3,1},{5,3},... | collective-permute-start | bytes 990728 | tf_op jit(solution)/shard_map/ppermute | solution.py:13
  34.6 20.8 %collective-permute-start.1 = (bf16[258,640]{1,0:T(8,128)(2,1)S(1)}, bf16[258,640]{1,0:T(8,128)(2,1)S(1)}, u32[]{:S(2)}, u32[]{:S(2)}) collective-permute-start(bf16[258,640]{1,0:T(8,128)(2,1)S(1)} %pad_maximum_fusion.2), channel_id=1, source_target_pairs={{4,0},{6,2},{8,4},{10,6},{12,8},{14,10},{0,12},{2,14},{5,1},{7,3},... | collective-permute-start | bytes 990728 | tf_op jit(solution)/shard_map/ppermute | solution.py:13
  54.8 14.1 %collective-permute-start = (bf16[258,640]{1,0:T(8,128)(2,1)S(1)}, bf16[258,640]{1,0:T(8,128)(2,1)S(1)}, u32[]{:S(2)}, u32[]{:S(2)}) collective-permute-start(bf16[258,640]{1,0:T(8,128)(2,1)S(1)} %pad_maximum_fusion.1), channel_id=1, source_target_pairs={{6,0},{8,2},{10,4},{12,6},{14,8},{0,10},{2,12},{4,14},{7,1},{9,3},... | collective-permute-start | bytes 990728 | tf_op jit(solution)/shard_map/ppermute | solution.py:13
where the time goes:
time: 74.1 us; the launch traced here: 73.9 us
  waiting for transfers between devices  32.1 us (43%)
  matrix products  13.4 us (18%)
  starting transfers between devices  10.7 us (14%)
  other arithmetic  7.68 us (10%)
  local copies, waits for them, and re-layouts  5.21 us (7%)
  blocking collectives  3.61 us (5%)
  between operations  1.22 us (2%)
    ppermute x6, waiting for transfers between devices, passed_along(): return lax.ppermute(block, axis, route)  32.1 us
    ppermute x6, starting transfers between devices, passed_along(): return lax.ppermute(block, axis, route)  10.7 us
    dot_general x6, matrix products, body(): jnp.einsum('j,ajtd->atd', picked, updated, preferred_element_type=jnp.flo...  4.96 us
    psum x1, blocking collectives, body(): resid = hidden.astype(jnp.float32) + lax.psum(partial_proj, 'mp')  3.61 us
    dot_general x1, matrix products, body(): jnp.einsum('jl,ajtd->altd', select, updated, preferred_element_type=jnp.f...  3.13 us
    unnamed x15, local copies, waits for them, and re-layouts  2.07 us
    dot_general x1, matrix products, body(): jnp.dot(normed, query_proj, preferred_element_type=jnp.float32)  1.79 us
  transfers between devices with their start and end apart: 6, of which 3 were waited for; matrix products, arithmetic and copies ran while one was open for 8% of the time, Pallas kernels for 0%

commit v1 on v0

v1 whole, which is shorter than its diff:
```python
import functools

import jax
import jax.numpy as jnp
from jax import lax
from jax.experimental import pallas as pl
from jax.experimental.pallas import tpu as pltpu
from jax.sharding import PartitionSpec as P

HEAD_DIM = 64
REACH = 3
MESH = pl.DeviceIdType.MESH
DISTANCES = [3, -3, 2, -2, 1, -1]


def attend(query, keys, values, length, own):
    slots, width = keys.shape
    heads = width // HEAD_DIM
    rows = -(-heads // 16) * 16
    row = lax.broadcasted_iota(jnp.int32, (rows, width), 0)
    column = lax.broadcasted_iota(jnp.int32, (rows, width), 1)
    low = row * HEAD_DIM
    mine = (column >= low) & (column < low + HEAD_DIM)
    spread = jnp.where(mine, query.astype(jnp.float32), 0.0)
    factor = HEAD_DIM ** (-0.5)
    scores = (
        lax.dot_general(
            spread.astype(jnp.bfloat16),
            keys,
            (((1,), (1,)), ((), ())),
            preferred_element_type=jnp.float32,
        )
        * factor
    )
    if length is not None:
        usable = lax.broadcasted_iota(jnp.int32, (rows, slots), 1) < length
        scores = jnp.where(usable, scores, -1e30)
    highest = jnp.max(scores, axis=-1, keepdims=True)
    if own is not None:
        new_key, new_value = own
        own_score = jnp.sum(spread * new_key.astype(jnp.float32), axis=-1, keepdims=True) * factor
        highest = jnp.maximum(highest, own_score)
    weight = jnp.exp(scores - highest)
    if length is not None:
        weight = jnp.where(usable, weight, 0.0)
    total = jnp.sum(weight, axis=-1, keepdims=True)
    if own is not None:
        own_weight = jnp.exp(own_score - highest)
        total = total + own_weight
    weight = (weight / total).astype(jnp.bfloat16)
    mixed = jnp.dot(weight, values, preferred_element_type=jnp.float32)
    if own is not None:
        own_weight = (own_weight / total).astype(jnp.bfloat16).astype(jnp.float32)
        mixed = mixed + own_weight * new_value.astype(jnp.float32)
    return jnp.sum(jnp.where(mine, mixed, 0.0), axis=0, keepdims=True)


def kernel(
    count,
    cores,
    cache_len,
    finished,
    new_slot,
    hidden,
    token_qkv,
    self_cache,
    ln_gain,
    ln_bias,
    cross_hbm,
    out_proj_hbm,
    query_proj_hbm,
    moved_cache,
    moved_out,
    cross,
    out_proj,
    query_proj,
    updated,
    parcel,
    arrived,
    mark,
    mark_in,
    line,
    line_in,
    part,
    part_in,
    load_sem,
    cache_sems,
    mark_sems,
    line_sems,
    part_sems,
):
    spans, width = hidden.shape
    slots, local = self_cache.shape[2:]
    me = lax.axis_index("batch")
    core = lax.axis_index("mp")
    loads = [
        pltpu.make_async_copy(source, target, load_sem.at[i])
        for i, (source, target) in enumerate(
            [(out_proj_hbm, out_proj), (query_proj_hbm, query_proj), (cross_hbm, cross)]
        )
    ]
    for load in loads:
        load.start()

    barrier = pltpu.get_barrier_semaphore()
    targets = [lax.rem(me + distance + count, count) for distance in DISTANCES]
    for target in targets:
        pl.semaphore_signal(barrier, inc=1, device_id={"batch": target}, device_id_type=MESH)
    others = [lax.rem(core + k, cores) for k in range(1, cores)]
    for other in others:
        pl.semaphore_signal(barrier, inc=1, device_id={"mp": other}, device_id_type=MESH)

    half = count // 2
    alive, offset, place = [], [], []
    for c in range(spans):
        slot = new_slot[c]
        owner = lax.div(slot, spans)
        offset.append(lax.rem(owner - me + half + count, count) - half)
        place.append(lax.rem(slot, spans))
        alive.append(jnp.where(finished[c] == 0, 1, 0))

    position = lax.broadcasted_iota(jnp.int32, (slots, local), 0)
    for c in range(spans):
        length = cache_len[c]
        older = jnp.where(position < length * alive[c], 1.0, 0.0).astype(jnp.bfloat16)
        fresh = jnp.where(position == jnp.where(alive[c] == 1, length, -1), 1.0, 0.0).astype(
            jnp.bfloat16
        )
        for a in range(2):
            updated[a, c] = self_cache[a, c] * older + token_qkv[1 + a, c : c + 1, :] * fresh

    def flag(value, shape):
        return jnp.full(shape, jnp.where(value, 1.0, 0.0), jnp.float32).astype(jnp.bfloat16)

    marker_row = lax.broadcasted_iota(jnp.int32, mark.shape[1:], 0)
    for i, distance in enumerate(DISTANCES):
        marker = jnp.zeros(mark.shape[1:], jnp.float32)
        for c in range(spans):
            at = jnp.where(offset[c] == distance, place[c], -1)
            marker = jnp.where(marker_row == at, 1.0, marker)
        mark[i] = marker.astype(jnp.bfloat16)

    def send(source, target, sems, i, distance):
        return pltpu.make_async_remote_copy(
            src_ref=source,
            dst_ref=target,
            send_sem=sems.at[0, i],
            recv_sem=sems.at[1, i],
            device_id={"batch": targets[i]},
            device_id_type=MESH,
        )

    pl.semaphore_wait(barrier, len(targets) + len(others))
    mark_copies, cache_copies = [], []
    for i, distance in enumerate(DISTANCES):
        copy = send(mark.at[i], mark_in.at[i], mark_sems, i, distance)
        copy.start()
        mark_copies.append(copy)
    for i, distance in enumerate(DISTANCES):
        for a in range(2):
            total = updated[a, 0] * flag(offset[0] == distance, (1, local))
            for c in range(1, spans):
                total = total + updated[a, c] * flag(offset[c] == distance, (1, local))
            parcel[i, a] = total
        copy = send(parcel.at[i], arrived.at[i], cache_sems, i, distance)
        copy.start()
        cache_copies.append(copy)

    for l in range(spans):
        for a in range(2):
            total = updated[a, 0] * flag((offset[0] == 0) & (place[0] == l), (1, local))
            for c in range(1, spans):
                keep = flag((offset[c] == 0) & (place[c] == l), (1, local))
                total = total + updated[a, c] * keep
            moved_cache[a, l] = total

    contexts = []
    for c in range(spans):
        query, key, value = (token_qkv[k, c : c + 1, :] for k in range(3))
        contexts.append(
            attend(query, self_cache[0, c], self_cache[1, c], cache_len[c], (key, value))
        )
    pad = part.shape[0] - spans
    context = jnp.concatenate(contexts + [jnp.zeros((pad, local), jnp.float32)], 0)
    context = context.astype(jnp.bfloat16)
    loads[0].wait()
    part[...] = jnp.dot(context, out_proj[...], preferred_element_type=jnp.float32)
    part_copies = []
    for k, other in enumerate(others):
        copy = pltpu.make_async_remote_copy(
            src_ref=part,
            dst_ref=part_in.at[k],
            send_sem=part_sems.at[0, k],
            recv_sem=part_sems.at[1, k],
            device_id={"mp": other},
            device_id_type=MESH,
        )
        copy.start()
        part_copies.append(copy)
    loads[1].wait()
    loads[2].wait()
    for copy in part_copies:
        copy.wait()
    summed = part[...]
    for k in range(len(others)):
        summed = summed + part_in[k]
    resid = hidden[...].astype(jnp.float32) + summed[:spans]
    centre = jnp.mean(resid, axis=-1, keepdims=True)
    spread = jnp.mean((resid - centre) ** 2, axis=-1, keepdims=True)
    gain = ln_gain[...].reshape(1, width)
    bias = ln_bias[...].reshape(1, width)
    normed = (resid - centre) * lax.rsqrt(spread + 1e-05) * gain + bias
    normed = jnp.concatenate([normed, jnp.zeros((pad, width), jnp.float32)], 0)
    query = jnp.dot(
        normed.astype(jnp.bfloat16), query_proj[...], preferred_element_type=jnp.float32
    ).astype(jnp.bfloat16).astype(jnp.float32)
    decoded = []
    for c in range(spans):
        mixed = attend(query[c : c + 1], cross[0, c], cross[1, c], None, None)
        decoded.append(mixed * jnp.where(alive[c] == 1, 1.0, 0.0))

    line_copies = []
    blank = jnp.zeros((line.shape[1] - 1, local), jnp.float32)
    for i, distance in enumerate(DISTANCES):
        row = jnp.zeros((1, local), jnp.float32)
        for c in range(spans):
            row = row + decoded[c] * jnp.where(offset[c] == distance, 1.0, 0.0)
        line[i] = jnp.concatenate([row, blank], 0).astype(jnp.bfloat16)
        copy = send(line.at[i], line_in.at[i], line_sems, i, distance)
        copy.start()
        line_copies.append(copy)

    rows = []
    for l in range(spans):
        row = jnp.zeros((1, local), jnp.float32)
        for c in range(spans):
            keep = (offset[c] == 0) & (place[c] == l)
            row = row + decoded[c] * jnp.where(keep, 1.0, 0.0)
        rows.append(row)
    for i in range(len(DISTANCES)):
        mark_copies[i].wait()
        cache_copies[i].wait()
        for l in range(spans):
            taken = mark_in[i, l : l + 1, :]
            for a in range(2):
                moved_cache[a, l] = moved_cache[a, l] + arrived[i, a] * taken
    for i in range(len(DISTANCES)):
        line_copies[i].wait()
        for l in range(spans):
            taken = mark_in[i, l : l + 1, :].astype(jnp.float32)
            rows[l] = rows[l] + line_in[i, 0:1, :].astype(jnp.float32) * taken
    moved_out[...] = jnp.concatenate(rows, 0).astype(jnp.bfloat16)


def body(
    hidden,
    token_qkv,
    self_cache,
    cross_kv,
    cache_len,
    finished,
    new_slot,
    out_proj,
    ln_gain,
    ln_bias,
    query_proj,
):
    count, cores = lax.axis_size("batch"), lax.axis_size("mp")
    spans, width = hidden.shape
    slots, local = self_cache.shape[2:]
    moves = len(DISTANCES)
    smem = pl.BlockSpec(memory_space=pltpu.SMEM)
    vmem = pl.BlockSpec(memory_space=pltpu.VMEM)
    away = pl.BlockSpec(memory_space=pl.ANY)
    bf16, f32 = jnp.bfloat16, jnp.float32
    return pl.pallas_call(
        functools.partial(kernel, count, cores),
        out_shape=(
            jax.ShapeDtypeStruct(self_cache.shape, bf16),
            jax.ShapeDtypeStruct((spans, local), bf16),
        ),
        in_specs=[smem] * 3 + [vmem] * 5 + [away] * 3,
        out_specs=(vmem, vmem),
        scratch_shapes=[
            pltpu.VMEM(cross_kv.shape, bf16),
            pltpu.VMEM(out_proj.shape, bf16),
            pltpu.VMEM(query_proj.shape, bf16),
            pltpu.VMEM(self_cache.shape, bf16),
            pltpu.VMEM((moves, 2, slots, local), bf16),
            pltpu.VMEM((moves, 2, slots, local), bf16),
            pltpu.VMEM((moves, 16, local), bf16),
            pltpu.VMEM((moves, 16, local), bf16),
            pltpu.VMEM((moves, 16, local), bf16),
            pltpu.VMEM((moves, 16, local), bf16),
            pltpu.VMEM((8, width), f32),
            pltpu.VMEM((cores - 1, 8, width), f32),
            pltpu.SemaphoreType.DMA((3,)),
            pltpu.SemaphoreType.DMA((2, moves)),
            pltpu.SemaphoreType.DMA((2, moves)),
            pltpu.SemaphoreType.DMA((2, moves)),
            pltpu.SemaphoreType.DMA((2, cores - 1)),
        ],
        compiler_params=pltpu.CompilerParams(collective_id=0, has_side_effects=True),
    )(
        cache_len,
        finished,
        new_slot,
        hidden,
        token_qkv,
        self_cache,
        ln_gain,
        ln_bias,
        cross_kv,
        out_proj,
        query_proj,
    )


def solution(mesh):
    placed = (
        P(("groups", "batch"), None),
        P(None, ("groups", "batch"), "mp"),
        P(None, ("groups", "batch"), None, "mp"),
        P(None, ("groups", "batch"), None, "mp"),
        P(("groups", "batch")),
        P(("groups", "batch")),
        P(("groups", "batch")),
        P("mp", None),
        P(),
        P(),
        P(None, "mp"),
    )
    return jax.shard_map(
        body,
        mesh=mesh,
        in_specs=placed,
        out_specs=(P(None, ("groups", "batch"), None, "mp"), P(("groups", "batch"), "mp")),
        check_vma=False,
    )
```

time: 74.1 us -> 60.7 us (0.82)
  Pallas kernels: 0 us -> 56.6 us
  waiting for transfers between devices: 32.1 us -> 0 us
  matrix products: 13.4 us -> 0 us
  starting transfers between devices: 10.7 us -> 0 us
  other arithmetic: 7.68 us -> 0 us
  blocking collectives: 3.61 us -> 0 us
  local copies, waits for them, and re-layouts: 5.21 us -> 3.23 us
    pallas_call x0 -> x1, Pallas kernels: none -> 56.6 us  [body(): pl.pallas_call(functools.partial(kernel, count, cores), out_shape=(jax.Sh...]
    ppermute x6 -> x0, waiting for transfers between devices: 32.1 us -> none  [passed_along(): return lax.ppermute(block, axis, route)]
    dot_general x26 -> x0, matrix products: 13.4 us -> none  [the longest x6 4.96 us: body(): jnp.einsum('j,ajtd->atd', picked, updated, preferred_element_type=jnp.flo...]
    ppermute x6 -> x0, starting transfers between devices: 10.7 us -> none  [passed_along(): return lax.ppermute(block, axis, route)]
    psum x1 -> x0, blocking collectives: 3.61 us -> none  [body(): resid = hidden.astype(jnp.float32) + lax.psum(partial_proj, 'mp')]
    select_n x2 -> x0, other arithmetic: 2.11 us -> none  [the longest x1 1.44 us: extend(): return jnp.where(alive[:, None, None], grown, jnp.zeros_like(older))]
    eq x3 -> x0, other arithmetic: 2.02 us -> none  [the longest x1 0.68 us: extend(): slot_pos == length]
    slice x10 -> x0, local copies, waits for them, and re-layouts: 1.72 us -> none  [the longest x1 1.05 us: body(): cross_keys = cross_kv[0].reshape(spans, frames, head_count, HEAD_DIM)]
  transfers between devices with their start and end apart: 6 -> 0, of which waited for: 3 -> 0; matrix products, arithmetic and copies ran while one was open for 8% -> 0% of each run, Pallas kernels for 0% -> 0%
where the time goes in v1:
time: 60.7 us; the launch traced here: 60.5 us
  Pallas kernels  56.6 us (93%)
  local copies, waits for them, and re-layouts  3.23 us (5%)
  between operations  0.64 us (1%)
    pallas_call x1, Pallas kernels, body(): pl.pallas_call(functools.partial(kernel, count, cores), out_shape=(jax.Sh...  56.6 us
    unnamed x2, local copies, waits for them, and re-layouts  3.23 us

profile of v1, /device:TPU:0, one launch (start us, length us, event | category | flops | bytes accessed | tf_op | source)
XLA Modules:
  0.0 60.5 jit_solution(18125622680898648491)
XLA Ops:
  0.6 56.6 %shard_map.122 = (bf16[2,2,128,640]{3,2,1,0:T(8,128)(2,1)}, bf16[2,640]{1,0:T(2,128)(2,1)}) custom-call(s32[2]{0:T(128)} %cache_len.1, s32[2]{0:T(128)} %finished.1, s32[2]{0:T(128)} %new_slot.1, bf16[2,1280]{1,0:T(2,128)(2,1)} %hidden.1, bf16[3,2,640]{2,1,0:T(2,128)(2,1)} %token_qkv.1, bf16[2,2,128,640]{3,2,1,0:T(8,128)(2,1)} %self_cache.1, f32[1280]{0:T(1024)} %ln_gain.1, ...), custom_call_target="tpu_custom_call" | custom-call | tf_op jit(solution)/shard_map/pallas_call | solution.py:276
  57.3 2.0 %copy.15 = bf16[2,2,128,640]{3,2,1,0:T(8,128)(2,1)} copy(bf16[2,2,128,640]{3,2,1,0:T(8,128)(2,1)} %get-tuple-element.4) | data formatting | bytes 1310720
  59.2 1.2 %copy.16 = bf16[2,640]{1,0:T(2,128)(2,1)} copy(bf16[2,640]{1,0:T(2,128)(2,1)} %get-tuple-element.5) | data formatting | bytes 5120

commit v2 on v1

--- a/solution.py
+++ b/solution.py
@@ -11,6 +11,9 @@
 REACH = 3
 MESH = pl.DeviceIdType.MESH
 DISTANCES = [3, -3, 2, -2, 1, -1]
+ROWS = 16
+LAG = 3
+EARLY = 1
 
 
 def attend(query, keys, values, length, own):
@@ -252,6 +255,346 @@
     moved_out[...] = jnp.concatenate(rows, 0).astype(jnp.bfloat16)
 
 
+def relay_kernel(
+    count,
+    cores,
+    cache_len,
+    finished,
+    new_slot,
+    hidden,
+    token_qkv,
+    self_cache,
+    ln_gain,
+    ln_bias,
+    cross_hbm,
+    out_proj_hbm,
+    query_proj_hbm,
+    moved_cache,
+    moved_out,
+    cross,
+    out_proj,
+    query_proj,
+    own,
+    raw_in,
+    cross_out,
+    cross_in,
+    kept,
+    final_out,
+    final_in,
+    pick,
+    label,
+    label_in,
+    mark,
+    mark_in,
+    line,
+    line_in,
+    part,
+    part_in,
+    load_sem,
+    raw_send,
+    raw_recv,
+    hop_sems,
+    label_send,
+    label_recv,
+    mark_sems,
+    line_sems,
+    part_sems,
+):
+    spans, width = hidden.shape
+    slots, local = self_cache.shape[2:]
+    steps, _, rows_per, _ = own.shape
+    per = steps // 2
+    me = lax.axis_index("batch")
+    core = lax.axis_index("mp")
+    level, column = lax.div(me, 2), lax.rem(me, 2)
+    left = level < REACH - 1
+    inner = (level == 1) | (level == REACH - 1)
+    outer = jnp.logical_not(inner)
+    loads = [
+        pltpu.make_async_copy(source, target, load_sem.at[i])
+        for i, (source, target) in enumerate(
+            [(out_proj_hbm, out_proj), (query_proj_hbm, query_proj), (cross_hbm, cross)]
+        )
+    ]
+    for load in loads:
+        load.start()
+
+    barrier = pltpu.get_barrier_semaphore()
+    targets = [lax.rem(me + distance + count, count) for distance in DISTANCES]
+    for target in targets:
+        pl.semaphore_signal(barrier, inc=1, device_id={"batch": target}, device_id_type=MESH)
+    others = [lax.rem(core + k, cores) for k in range(1, cores)]
+    for other in others:
+        pl.semaphore_signal(barrier, inc=1, device_id={"mp": other}, device_id_type=MESH)
+
+    mate_level = jnp.where(level == 0, 1, jnp.where(level == 1, 0, jnp.where(level == 2, 3, 2)))
+    mate = mate_level * 2 + column
+    mate_aside = mate_level * 2 + 1 - column
+    aside = level * 2 + 1 - column
+    across = (REACH - level) * 2 + column
+    beyond = (REACH - mate_level) * 2 + column
+
+    half = count // 2
+    alive, offset, place = [], [], []
+    for c in range(spans):
+        slot = new_slot[c]
+        owner = lax.div(slot, spans)
+        offset.append(lax.rem(owner - me + half + count, count) - half)
+        place.append(lax.rem(slot, spans))
+        alive.append(jnp.where(finished[c] == 0, 1, 0))
+
+    def to(node, source, target, sent, received):
+        return pltpu.make_async_remote_copy(
+            src_ref=source,
+            dst_ref=target,
+            send_sem=sent,
+            recv_sem=received,
+            device_id={"batch": node},
+            device_id_type=MESH,
+        )
+
+    def raw_copy(node, lane, way, k):
+        return to(node, own.at[k], raw_in.at[way, k], raw_send.at[lane, k], raw_recv.at[way, k])
+
+    def cross_copy(k):
+        return to(across, cross_out.at[k], cross_in.at[k], hop_sems.at[0, k], hop_sems.at[1, k])
+
+    def final_copy(k):
+        return to(mate, final_out.at[k], final_in.at[k], hop_sems.at[2, k], hop_sems.at[3, k])
+
+    def label_copy(node, lane, way):
+        return to(node, label, label_in.at[way], label_send.at[lane], label_recv.at[way])
+
+    def mark_copy(i):
+        return to(targets[i], mark.at[i], mark_in.at[i], mark_sems.at[0, i], mark_sems.at[1, i])
+
+    def line_copy(i):
+        return to(targets[i], line.at[i], line_in.at[i], line_sems.at[0, i], line_sems.at[1, i])
+
+    label_row = lax.broadcasted_iota(jnp.int32, label.shape, 0)
+    labels = jnp.zeros(label.shape, jnp.int32)
+    for c in range(spans):
+        labels = jnp.where(label_row == c, new_slot[c], labels)
+    label[...] = labels.astype(jnp.float32)
+    marker_row = lax.broadcasted_iota(jnp.int32, mark.shape[1:], 0)
+    for i, distance in enumerate(DISTANCES):
+        marker = jnp.zeros(mark.shape[1:], jnp.float32)
+        for c in range(spans):
+            at = jnp.where(offset[c] == distance, place[c], -1)
+            marker = jnp.where(marker_row == at, 1.0, marker)
+        mark[i] = marker.astype(jnp.bfloat16)
+
+    pl.semaphore_wait(barrier, len(targets) + len(others))
+
+    position = lax.broadcasted_iota(jnp.int32, (rows_per, local), 0)
+    ends = [cache_len[c] * alive[c] for c in range(spans)]
+    fresh_at = [jnp.where(alive[c] == 1, cache_len[c], -1) for c in range(spans)]
+
+    def grow(k, _):
+        a, r = lax.div(k, per), lax.rem(k, per)
+        start = pl.multiple_of(r * rows_per, rows_per)
+        at = position + start
+        for c in range(spans):
+            older = jnp.where(at < ends[c], 1.0, 0.0).astype(jnp.bfloat16)
+            fresh = jnp.where(at == fresh_at[c], 1.0, 0.0).astype(jnp.bfloat16)
+            new = jnp.where(a == 0, token_qkv[1, c : c + 1, :].astype(jnp.float32),
+                            token_qkv[2, c : c + 1, :].astype(jnp.float32)).astype(jnp.bfloat16)
+            own[k, c] = self_cache[a, c, pl.ds(start, rows_per), :] * older + new * fresh
+
+        @pl.when(outer)
+        def _():
+            raw_copy(mate, 0, 0, k).start()
+            raw_copy(mate_aside, 1, 1, k).start()
+
+        @pl.when(inner)
+        def _():
+            raw_copy(aside, 0, 2, k).start()
+
+        return 0
+
+    @pl.when(outer)
+    def _():
+        label_copy(mate, 0, 0).start()
+        label_copy(mate_aside, 1, 1).start()
+
+    @pl.when(inner)
+    def _():
+        label_copy(aside, 0, 2).start()
+
+    lax.fori_loop(0, steps, grow, 0)
+    for i in range(len(DISTANCES)):
+        mark_copy(i).start()
+
+    def self_part():
+        contexts = []
+        for c in range(spans):
+            query, key, value = (token_qkv[k, c : c + 1, :] for k in range(3))
+            contexts.append(
+                attend(query, self_cache[0, c], self_cache[1, c], cache_len[c], (key, value))
+            )
+        context = jnp.concatenate(contexts + [jnp.zeros((pad, local), jnp.float32)], 0)
+        context = context.astype(jnp.bfloat16)
+        loads[0].wait()
+        part[...] = jnp.dot(context, out_proj[...], preferred_element_type=jnp.float32)
+
+    def part_copy(k):
+        return pltpu.make_async_remote_copy(
+            src_ref=part,
+            dst_ref=part_in.at[k],
+            send_sem=part_sems.at[0, k],
+            recv_sem=part_sems.at[1, k],
+            device_id={"mp": others[k]},
+            device_id_type=MESH,
+        )
+
+    pad = part.shape[0] - spans
+    self_part()
+    for k in range(len(others)):
+        part_copy(k).start()
+
+    @pl.when(inner)
+    def _():
+        for way in range(3):
+            label_copy(mate, 0, way).wait_recv()
+        sources = [label] + [label_in.at[way] for way in range(3)]
+        nodes = [me, mate, across, beyond]
+        for s, source in enumerate(sources):
+            for c in range(spans):
+                held = jnp.broadcast_to(source[c : c + 1, :], (rows_per, local))
+                for d, node in enumerate(nodes):
+                    for l in range(spans):
+                        wanted = jnp.full((rows_per, local), node * spans + l, jnp.int32)
+                        pick[s * spans + c, d * spans + l] = jnp.where(
+                            held == wanted.astype(jnp.float32), 1.0, 0.0
+                        ).astype(jnp.bfloat16)
+
+    def merge(k, _):
+        for way in range(3):
+            raw_copy(mate, 0, way, k).wait_recv()
+        blocks = [own[k, c] for c in range(spans)]
+        for way in range(3):
+            blocks += [raw_in[way, k, c] for c in range(spans)]
+
+        def gathered(d):
+            total = blocks[0] * pick[0, d]
+            for s in range(1, len(blocks)):
+                total = total + blocks[s] * pick[s, d]
+            return total
+
+        for d in range(2 * spans):
+            cross_out[k, d] = gathered(2 * spans + d)
+        cross_copy(k).start()
+        for d in range(2 * spans):
+            kept[k, d] = gathered(d)
+        return 0
+
+    def finish(k, _):
+        cross_copy(k).wait_recv()
+        a, r = lax.div(k, per), lax.rem(k, per)
+        start = pl.multiple_of(r * rows_per, rows_per)
+        for l in range(spans):
+            final_out[k, l] = kept[k, spans + l] + cross_in[k, spans + l]
+        final_copy(k).start()
+        for l in range(spans):
+            moved_cache[a, l, pl.ds(start, rows_per), :] = kept[k, l] + cross_in[k, l]
+        return 0
+
+    def both(k, _):
+        merge(k, 0)
+        finish(k - LAG, 0)
+        return 0
+
+    @pl.when(inner)
+    def _():
+        lax.fori_loop(0, EARLY, merge, 0)
+
+    loads[1].wait()
+    loads[2].wait()
+    for k in range(len(others)):
+        part_copy(k).wait()
+    summed = part[...]
+    for k in range(len(others)):
+        summed = summed + part_in[k]
+    resid = hidden[...].astype(jnp.float32) + summed[:spans]
+    centre = jnp.mean(resid, axis=-1, keepdims=True)
+    spread = jnp.mean((resid - centre) ** 2, axis=-1, keepdims=True)
+    gain = ln_gain[...].reshape(1, width)
+    bias = ln_bias[...].reshape(1, width)
+    normed = (resid - centre) * lax.rsqrt(spread + 1e-05) * gain + bias
+    normed = jnp.concatenate([normed, jnp.zeros((pad, width), jnp.float32)], 0)
+    query = jnp.dot(
+        normed.astype(jnp.bfloat16), query_proj[...], preferred_element_type=jnp.float32
+    ).astype(jnp.bfloat16).astype(jnp.float32)
+
+    @pl.when(inner)
+    def _():
+        lax.fori_loop(EARLY, LAG, merge, 0)
+
+    decoded = []
+    for c in range(spans):
+        mixed = attend(query[c : c + 1], cross[0, c], cross[1, c], None, None)
+        decoded.append(mixed * jnp.where(alive[c] == 1, 1.0, 0.0))
+
+    blank = jnp.zeros((line.shape[1] - 1, local), jnp.float32)
+    for i, distance in enumerate(DISTANCES):
+        row = jnp.zeros((1, local), jnp.float32)
+        for c in range(spans):
+            row = row + decoded[c] * jnp.where(offset[c] == distance, 1.0, 0.0)
+        line[i] = jnp.concatenate([row, blank], 0).astype(jnp.bfloat16)
+        line_copy(i).start()
+
+    @pl.when(inner)
+    def _():
+        lax.fori_loop(LAG, steps, both, 0)
+
+    rows = []
+    for l in range(spans):
+        row = jnp.zeros((1, local), jnp.float32)
+        for c in range(spans):
+            keep = (offset[c] == 0) & (place[c] == l)
+            row = row + decoded[c] * jnp.where(keep, 1.0, 0.0)
+        rows.append(row)
+    for i in range(len(DISTANCES)):
+        mark_copy(i).wait()
+        line_copy(i).wait()
+        for l in range(spans):
+            taken = mark_in[i, l : l + 1, :].astype(jnp.float32)
+            rows[l] = rows[l] + line_in[i, 0:1, :].astype(jnp.float32) * taken
+    moved_out[...] = jnp.concatenate(rows, 0).astype(jnp.bfloat16)
+
+    def land(k, _):
+        final_copy(k).wait_recv()
+        a, r = lax.div(k, per), lax.rem(k, per)
+        start = pl.multiple_of(r * rows_per, rows_per)
+        for l in range(spans):
+            moved_cache[a, l, pl.ds(start, rows_per), :] = final_in[k, l]
+        return 0
+
+    def outer_sent(k, _):
+        raw_copy(mate, 0, 0, k).wait_send()
+        raw_copy(mate_aside, 1, 1, k).wait_send()
+        return 0
+
+    def inner_sent(k, _):
+        raw_copy(aside, 0, 2, k).wait_send()
+        cross_copy(k).wait_send()
+        final_copy(k).wait_send()
+        return 0
+
+    @pl.when(inner)
+    def _():
+        lax.fori_loop(steps - LAG, steps, finish, 0)
+        label_copy(aside, 0, 2).wait_send()
+        lax.fori_loop(0, steps, inner_sent, 0)
+
+    @pl.when(outer)
+    def _():
+        lax.fori_loop(0, steps, land, 0)
+        label_copy(mate, 0, 0).wait_send()
+        label_copy(mate_aside, 1, 1).wait_send()
+        lax.fori_loop(0, steps, outer_sent, 0)
+
+
 def body(
     hidden,
     token_qkv,
@@ -273,35 +616,7 @@
     vmem = pl.BlockSpec(memory_space=pltpu.VMEM)
     away = pl.BlockSpec(memory_space=pl.ANY)
     bf16, f32 = jnp.bfloat16, jnp.float32
-    return pl.pallas_call(
-        functools.partial(kernel, count, cores),
-        out_shape=(
-            jax.ShapeDtypeStruct(self_cache.shape, bf16),
-            jax.ShapeDtypeStruct((spans, local), bf16),
-        ),
-        in_specs=[smem] * 3 + [vmem] * 5 + [away] * 3,
-        out_specs=(vmem, vmem),
-        scratch_shapes=[
-            pltpu.VMEM(cross_kv.shape, bf16),
-            pltpu.VMEM(out_proj.shape, bf16),
-            pltpu.VMEM(query_proj.shape, bf16),
-            pltpu.VMEM(self_cache.shape, bf16),
-            pltpu.VMEM((moves, 2, slots, local), bf16),
-            pltpu.VMEM((moves, 2, slots, local), bf16),
-            pltpu.VMEM((moves, 16, local), bf16),
-            pltpu.VMEM((moves, 16, local), bf16),
-            pltpu.VMEM((moves, 16, local), bf16),
-            pltpu.VMEM((moves, 16, local), bf16),
-            pltpu.VMEM((8, width), f32),
-            pltpu.VMEM((cores - 1, 8, width), f32),
-            pltpu.SemaphoreType.DMA((3,)),
-            pltpu.SemaphoreType.DMA((2, moves)),
-            pltpu.SemaphoreType.DMA((2, moves)),
-            pltpu.SemaphoreType.DMA((2, moves)),
-            pltpu.SemaphoreType.DMA((2, cores - 1)),
-        ],
-        compiler_params=pltpu.CompilerParams(collective_id=0, has_side_effects=True),
-    )(
+    operands = (
         cache_len,
         finished,
         new_slot,
@@ -314,6 +629,72 @@
         out_proj,
         query_proj,
     )
+    parcels = pltpu.VMEM((moves, 2, slots, local), bf16)
+    tiles = pltpu.VMEM((moves, 16, local), bf16)
+    dma = pltpu.SemaphoreType.DMA
+    inputs = [pltpu.VMEM(array.shape, bf16) for array in (cross_kv, out_proj, query_proj)]
+    parts = [pltpu.VMEM((8, width), f32), pltpu.VMEM((cores - 1, 8, width), f32)]
+    steps = 2 * slots // ROWS
+    if count == 2 * (REACH + 1):
+        function = relay_kernel
+
+        def blocks(*lead):
+            return pltpu.VMEM(lead + (ROWS, local), bf16)
+
+        scratch = inputs + [
+            blocks(steps, spans),
+            blocks(3, steps, spans),
+            blocks(steps, 2 * spans),
+            blocks(steps, 2 * spans),
+            blocks(steps, 2 * spans),
+            blocks(steps, spans),
+            blocks(steps, spans),
+            blocks(4 * spans, 4 * spans),
+            pltpu.VMEM((8, local), f32),
+            pltpu.VMEM((3, 8, local), f32),
+            tiles,
+            tiles,
+            tiles,
+            tiles,
+            *parts,
+            dma((3,)),
+            dma((2, steps)),
+            dma((3, steps)),
+            dma((4, steps)),
+            dma((2,)),
+            dma((3,)),
+            dma((2, moves)),
+            dma((2, moves)),
+            dma((2, cores - 1)),
+        ]
+    else:
+        function = kernel
+        scratch = inputs + [
+            pltpu.VMEM(self_cache.shape, bf16),
+            parcels,
+            parcels,
+            tiles,
+            tiles,
+            tiles,
+            tiles,
+            *parts,
+            dma((3,)),
+            dma((2, moves)),
+            dma((2, moves)),
+            dma((2, moves)),
+            dma((2, cores - 1)),
+        ]
+    return pl.pallas_call(
+        functools.partial(function, count, cores),
+        out_shape=(
+            jax.ShapeDtypeStruct(self_cache.shape, bf16),
+            jax.ShapeDtypeStruct((spans, local), bf16),
+        ),
+        in_specs=[smem] * 3 + [vmem] * 5 + [away] * 3,
+        out_specs=(vmem, vmem),
+        scratch_shapes=scratch,
+        compiler_params=pltpu.CompilerParams(collective_id=0, has_side_effects=True),
+    )(*operands)
 
 
 def solution(mesh):

time: 60.7 us -> 54.3 us (0.89)
  Pallas kernels: 56.6 us -> 50.2 us
    pallas_call x1, Pallas kernels: 56.6 us -> 50.2 us  [body(): pl.pallas_call(functools.partial(function, count, cores), out_shape=(jax....]
where the time goes in v2:
time: 54.3 us; the launch traced here: 54 us
  Pallas kernels  50.2 us (92%)
  local copies, waits for them, and re-layouts  3.23 us (6%)
  between operations  0.64 us (1%)
    pallas_call x1, Pallas kernels, body(): pl.pallas_call(functools.partial(function, count, cores), out_shape=(jax....  50.2 us
    unnamed x2, local copies, waits for them, and re-layouts  3.23 us

profile of v2, /device:TPU:0, one launch (start us, length us, event | category | flops | bytes accessed | tf_op | source)
XLA Modules:
  0.0 54.0 jit_solution(11720253701938928693)
XLA Ops:
  0.6 50.2 %shard_map.122 = (bf16[2,2,128,640]{3,2,1,0:T(8,128)(2,1)}, bf16[2,640]{1,0:T(2,128)(2,1)}) custom-call(s32[2]{0:T(128)} %cache_len.1, s32[2]{0:T(128)} %finished.1, s32[2]{0:T(128)} %new_slot.1, bf16[2,1280]{1,0:T(2,128)(2,1)} %hidden.1, bf16[3,2,640]{2,1,0:T(2,128)(2,1)} %token_qkv.1, bf16[2,2,128,640]{3,2,1,0:T(8,128)(2,1)} %self_cache.1, f32[1280]{0:T(1024)} %ln_gain.1, ...), custom_call_target="tpu_custom_call" | custom-call | tf_op jit(solution)/shard_map/pallas_call | solution.py:687
  50.8 2.0 %copy.15 = bf16[2,2,128,640]{3,2,1,0:T(8,128)(2,1)} copy(bf16[2,2,128,640]{3,2,1,0:T(8,128)(2,1)} %get-tuple-element.4) | data formatting | bytes 1310720
  52.8 1.2 %copy.16 = bf16[2,640]{1,0:T(2,128)(2,1)} copy(bf16[2,640]{1,0:T(2,128)(2,1)} %get-tuple-element.5) | data formatting | bytes 5120

commit v3 on v2

--- a/solution.py
+++ b/solution.py
@@ -284,8 +284,6 @@
     pick,
     label,
     label_in,
-    mark,
-    mark_in,
     line,
     line_in,
     part,
@@ -296,7 +294,6 @@
     hop_sems,
     label_send,
     label_recv,
-    mark_sems,
     line_sems,
     part_sems,
 ):
@@ -365,9 +362,6 @@
     def label_copy(node, lane, way):
         return to(node, label, label_in.at[way], label_send.at[lane], label_recv.at[way])
 
-    def mark_copy(i):
-        return to(targets[i], mark.at[i], mark_in.at[i], mark_sems.at[0, i], mark_sems.at[1, i])
-
     def line_copy(i):
         return to(targets[i], line.at[i], line_in.at[i], line_sems.at[0, i], line_sems.at[1, i])
 
@@ -376,13 +370,6 @@
     for c in range(spans):
         labels = jnp.where(label_row == c, new_slot[c], labels)
     label[...] = labels.astype(jnp.float32)
-    marker_row = lax.broadcasted_iota(jnp.int32, mark.shape[1:], 0)
-    for i, distance in enumerate(DISTANCES):
-        marker = jnp.zeros(mark.shape[1:], jnp.float32)
-        for c in range(spans):
-            at = jnp.where(offset[c] == distance, place[c], -1)
-            marker = jnp.where(marker_row == at, 1.0, marker)
-        mark[i] = marker.astype(jnp.bfloat16)
 
     pl.semaphore_wait(barrier, len(targets) + len(others))
 
@@ -422,8 +409,6 @@
         label_copy(aside, 0, 2).start()
 
     lax.fori_loop(0, steps, grow, 0)
-    for i in range(len(DISTANCES)):
-        mark_copy(i).start()
 
     def self_part():
         contexts = []
@@ -460,7 +445,7 @@
         nodes = [me, mate, across, beyond]
         for s, source in enumerate(sources):
             for c in range(spans):
-                held = jnp.broadcast_to(source[c : c + 1, :], (rows_per, local))
+                held = jnp.broadcast_to(source[c : c + 1, 0:1], (rows_per, local))
                 for d, node in enumerate(nodes):
                     for l in range(spans):
                         wanted = jnp.full((rows_per, local), node * spans + l, jnp.int32)
@@ -535,32 +520,29 @@
         mixed = attend(query[c : c + 1], cross[0, c], cross[1, c], None, None)
         decoded.append(mixed * jnp.where(alive[c] == 1, 1.0, 0.0))
 
-    blank = jnp.zeros((line.shape[1] - 1, local), jnp.float32)
+    def placed(distance):
+        rows = []
+        for l in range(spans):
+            row = jnp.zeros((1, local), jnp.float32)
+            for c in range(spans):
+                keep = (offset[c] == distance) & (place[c] == l)
+                row = row + decoded[c] * jnp.where(keep, 1.0, 0.0)
+            rows.append(row)
+        return jnp.concatenate(rows, 0)
+
     for i, distance in enumerate(DISTANCES):
-        row = jnp.zeros((1, local), jnp.float32)
-        for c in range(spans):
-            row = row + decoded[c] * jnp.where(offset[c] == distance, 1.0, 0.0)
-        line[i] = jnp.concatenate([row, blank], 0).astype(jnp.bfloat16)
+        line[i] = placed(distance).astype(jnp.bfloat16)
         line_copy(i).start()
 
     @pl.when(inner)
     def _():
         lax.fori_loop(LAG, steps, both, 0)
 
-    rows = []
-    for l in range(spans):
-        row = jnp.zeros((1, local), jnp.float32)
-        for c in range(spans):
-            keep = (offset[c] == 0) & (place[c] == l)
-            row = row + decoded[c] * jnp.where(keep, 1.0, 0.0)
-        rows.append(row)
+    total = placed(0)
     for i in range(len(DISTANCES)):
-        mark_copy(i).wait()
         line_copy(i).wait()
-        for l in range(spans):
-            taken = mark_in[i, l : l + 1, :].astype(jnp.float32)
-            rows[l] = rows[l] + line_in[i, 0:1, :].astype(jnp.float32) * taken
-    moved_out[...] = jnp.concatenate(rows, 0).astype(jnp.bfloat16)
+        total = total + line_in[i].astype(jnp.float32)
+    moved_out[...] = total.astype(jnp.bfloat16)
 
     def land(k, _):
         final_copy(k).wait_recv()
@@ -650,12 +632,10 @@
             blocks(steps, spans),
             blocks(steps, spans),
             blocks(4 * spans, 4 * spans),
-            pltpu.VMEM((8, local), f32),
-            pltpu.VMEM((3, 8, local), f32),
-            tiles,
-            tiles,
-            tiles,
-            tiles,
+            pltpu.VMEM((8, 128), f32),
+            pltpu.VMEM((3, 8, 128), f32),
+            pltpu.VMEM((moves, spans, local), bf16),
+            pltpu.VMEM((moves, spans, local), bf16),
             *parts,
             dma((3,)),
             dma((2, steps)),
@@ -663,7 +643,6 @@
             dma((4, steps)),
             dma((2,)),
             dma((3,)),
-            dma((2, moves)),
             dma((2, moves)),
             dma((2, cores - 1)),
         ]

time: 54.3 us -> 49.5 us (0.912)
  Pallas kernels: 50.2 us -> 45.5 us
    pallas_call x1, Pallas kernels: 50.2 us -> 45.5 us  [body(): pl.pallas_call(functools.partial(function, count, cores), out_shape=(jax....]
where the time goes in v3:
time: 49.5 us; the launch traced here: 49.3 us
  Pallas kernels  45.5 us (92%)
  local copies, waits for them, and re-layouts  3.23 us (7%)
  between operations  0.64 us (1%)
    pallas_call x1, Pallas kernels, body(): pl.pallas_call(functools.partial(function, count, cores), out_shape=(jax....  45.5 us
    unnamed x2, local copies, waits for them, and re-layouts  3.23 us

profile of v3, /device:TPU:0, one launch (start us, length us, event | category | flops | bytes accessed | tf_op | source)
XLA Modules:
  0.0 49.3 jit_solution(14377832649477169630)
XLA Ops:
  0.6 45.5 %shard_map.122 = (bf16[2,2,128,640]{3,2,1,0:T(8,128)(2,1)}, bf16[2,640]{1,0:T(2,128)(2,1)}) custom-call(s32[2]{0:T(128)} %cache_len.1, s32[2]{0:T(128)} %finished.1, s32[2]{0:T(128)} %new_slot.1, bf16[2,1280]{1,0:T(2,128)(2,1)} %hidden.1, bf16[3,2,640]{2,1,0:T(2,128)(2,1)} %token_qkv.1, bf16[2,2,128,640]{3,2,1,0:T(8,128)(2,1)} %self_cache.1, f32[1280]{0:T(1024)} %ln_gain.1, ...), custom_call_target="tpu_custom_call" | custom-call | tf_op jit(solution)/shard_map/pallas_call | solution.py:666
  46.1 2.0 %copy.15 = bf16[2,2,128,640]{3,2,1,0:T(8,128)(2,1)} copy(bf16[2,2,128,640]{3,2,1,0:T(8,128)(2,1)} %get-tuple-element.4) | data formatting | bytes 1310720
  48.1 1.2 %copy.16 = bf16[2,640]{1,0:T(2,128)(2,1)} copy(bf16[2,640]{1,0:T(2,128)(2,1)} %get-tuple-element.5) | data formatting | bytes 5120

commit v4 on v3

--- a/solution.py
+++ b/solution.py
@@ -14,6 +14,8 @@
 ROWS = 16
 LAG = 3
 EARLY = 1
+MIDDLE = 14
+HOLD = 8
 
 
 def attend(query, keys, values, length, own):
@@ -263,7 +265,7 @@
     new_slot,
     hidden,
     token_qkv,
-    self_cache,
+    cache_hbm,
     ln_gain,
     ln_bias,
     cross_hbm,
@@ -271,6 +273,7 @@
     query_proj_hbm,
     moved_cache,
     moved_out,
+    self_cache,
     cross,
     out_proj,
     query_proj,
@@ -286,6 +289,11 @@
     label_in,
     line,
     line_in,
+    line_kept,
+    line_out,
+    line_cross,
+    line_last,
+    line_final,
     part,
     part_in,
     load_sem,
@@ -294,7 +302,9 @@
     hop_sems,
     label_send,
     label_recv,
-    line_sems,
+    line_send,
+    line_recv,
+    line_hops,
     part_sems,
 ):
     spans, width = hidden.shape
@@ -304,25 +314,12 @@
     me = lax.axis_index("batch")
     core = lax.axis_index("mp")
     level, column = lax.div(me, 2), lax.rem(me, 2)
-    left = level < REACH - 1
     inner = (level == 1) | (level == REACH - 1)
     outer = jnp.logical_not(inner)
-    loads = [
-        pltpu.make_async_copy(source, target, load_sem.at[i])
-        for i, (source, target) in enumerate(
-            [(out_proj_hbm, out_proj), (query_proj_hbm, query_proj), (cross_hbm, cross)]
-        )
-    ]
-    for load in loads:
-        load.start()
-
     barrier = pltpu.get_barrier_semaphore()
-    targets = [lax.rem(me + distance + count, count) for distance in DISTANCES]
-    for target in targets:
-        pl.semaphore_signal(barrier, inc=1, device_id={"batch": target}, device_id_type=MESH)
-    others = [lax.rem(core + k, cores) for k in range(1, cores)]
-    for other in others:
-        pl.semaphore_signal(barrier, inc=1, device_id={"mp": other}, device_id_type=MESH)
+
+    def greet(where):
+        pl.semaphore_signal(barrier, inc=1, device_id=where, device_id_type=MESH)
 
     mate_level = jnp.where(level == 0, 1, jnp.where(level == 1, 0, jnp.where(level == 2, 3, 2)))
     mate = mate_level * 2 + column
@@ -330,15 +327,33 @@
     aside = level * 2 + 1 - column
     across = (REACH - level) * 2 + column
     beyond = (REACH - mate_level) * 2 + column
-
-    half = count // 2
-    alive, offset, place = [], [], []
-    for c in range(spans):
-        slot = new_slot[c]
-        owner = lax.div(slot, spans)
-        offset.append(lax.rem(owner - me + half + count, count) - half)
-        place.append(lax.rem(slot, spans))
-        alive.append(jnp.where(finished[c] == 0, 1, 0))
+    others = [lax.rem(core + k, cores) for k in range(1, cores)]
+    for node in (mate, mate_aside):
+        greet({"batch": node})
+
+    @pl.when(inner)
+    def _():
+        greet({"batch": aside})
+        greet({"batch": across})
+
+    for other in others:
+        greet({"mp": other})
+    loads = [
+        pltpu.make_async_copy(source, target, load_sem.at[i])
+        for i, (source, target) in enumerate(
+            [
+                (out_proj_hbm, out_proj),
+                (query_proj_hbm, query_proj),
+                (cross_hbm, cross),
+                (cache_hbm.at[0], self_cache.at[0]),
+                (cache_hbm.at[1], self_cache.at[1]),
+            ]
+        )
+    ]
+    for i in (3, 4, 0, 1, 2):
+        loads[i].start()
+
+    alive = [jnp.where(finished[c] == 0, 1, 0) for c in range(spans)]
 
     def to(node, source, target, sent, received):
         return pltpu.make_async_remote_copy(
@@ -353,17 +368,30 @@
     def raw_copy(node, lane, way, k):
         return to(node, own.at[k], raw_in.at[way, k], raw_send.at[lane, k], raw_recv.at[way, k])
 
-    def cross_copy(k):
-        return to(across, cross_out.at[k], cross_in.at[k], hop_sems.at[0, k], hop_sems.at[1, k])
+    def cross_copy(k, part):
+        first = (1 - part) * spans
+        return to(
+            across,
+            cross_out.at[k, pl.ds(first, spans)],
+            cross_in.at[k, pl.ds(first, spans)],
+            hop_sems.at[2 * part, k],
+            hop_sems.at[2 * part + 1, k],
+        )
 
     def final_copy(k):
-        return to(mate, final_out.at[k], final_in.at[k], hop_sems.at[2, k], hop_sems.at[3, k])
+        return to(mate, final_out.at[k], final_in.at[k], hop_sems.at[4, k], hop_sems.at[5, k])
 
     def label_copy(node, lane, way):
         return to(node, label, label_in.at[way], label_send.at[lane], label_recv.at[way])
 
-    def line_copy(i):
-        return to(targets[i], line.at[i], line_in.at[i], line_sems.at[0, i], line_sems.at[1, i])
+    def line_copy(node, lane, way):
+        return to(node, line, line_in.at[way], line_send.at[lane], line_recv.at[way])
+
+    def line_cross_copy():
+        return to(across, line_out, line_cross, line_hops.at[0], line_hops.at[1])
+
+    def line_final_copy():
+        return to(mate, line_last, line_final, line_hops.at[2], line_hops.at[3])
 
     label_row = lax.broadcasted_iota(jnp.int32, label.shape, 0)
     labels = jnp.zeros(label.shape, jnp.int32)
@@ -371,7 +399,13 @@
         labels = jnp.where(label_row == c, new_slot[c], labels)
     label[...] = labels.astype(jnp.float32)
 
-    pl.semaphore_wait(barrier, len(targets) + len(others))
+    @pl.when(inner)
+    def _():
+        pl.semaphore_wait(barrier, 4 + len(others))
+
+    @pl.when(outer)
+    def _():
+        pl.semaphore_wait(barrier, 2 + len(others))
 
     position = lax.broadcasted_iota(jnp.int32, (rows_per, local), 0)
     ends = [cache_len[c] * alive[c] for c in range(spans)]
@@ -388,6 +422,9 @@
                             token_qkv[2, c : c + 1, :].astype(jnp.float32)).astype(jnp.bfloat16)
             own[k, c] = self_cache[a, c, pl.ds(start, rows_per), :] * older + new * fresh
 
+        return 0
+
+    def pass_on(k, _):
         @pl.when(outer)
         def _():
             raw_copy(mate, 0, 0, k).start()
@@ -399,6 +436,11 @@
 
         return 0
 
+    def grow_and_pass(k, _):
+        grow(k, 0)
+        pass_on(k, 0)
+        return 0
+
     @pl.when(outer)
     def _():
         label_copy(mate, 0, 0).start()
@@ -408,7 +450,11 @@
     def _():
         label_copy(aside, 0, 2).start()
 
-    lax.fori_loop(0, steps, grow, 0)
+    loads[3].wait()
+    lax.fori_loop(0, per, grow_and_pass, 0)
+    loads[4].wait()
+    lax.fori_loop(per, HOLD, grow_and_pass, 0)
+    lax.fori_loop(HOLD, steps, grow, 0)
 
     def self_part():
         contexts = []
@@ -466,20 +512,22 @@
                 total = total + blocks[s] * pick[s, d]
             return total
 
-        for d in range(2 * spans):
-            cross_out[k, d] = gathered(2 * spans + d)
-        cross_copy(k).start()
+        for part in range(2):
+            for d in range((1 - part) * spans, (2 - part) * spans):
+                cross_out[k, d] = gathered(2 * spans + d)
+            cross_copy(k, part).start()
         for d in range(2 * spans):
             kept[k, d] = gathered(d)
         return 0
 
     def finish(k, _):
-        cross_copy(k).wait_recv()
+        cross_copy(k, 0).wait_recv()
         a, r = lax.div(k, per), lax.rem(k, per)
         start = pl.multiple_of(r * rows_per, rows_per)
         for l in range(spans):
             final_out[k, l] = kept[k, spans + l] + cross_in[k, spans + l]
         final_copy(k).start()
+        cross_copy(k, 1).wait_recv()
         for l in range(spans):
             moved_cache[a, l, pl.ds(start, rows_per), :] = kept[k, l] + cross_in[k, l]
         return 0
@@ -520,29 +568,42 @@
         mixed = attend(query[c : c + 1], cross[0, c], cross[1, c], None, None)
         decoded.append(mixed * jnp.where(alive[c] == 1, 1.0, 0.0))
 
-    def placed(distance):
+    line[...] = jnp.concatenate(decoded, 0).astype(jnp.bfloat16)
+
+    @pl.when(outer)
+    def _():
+        line_copy(mate, 0, 0).start()
+        line_copy(mate_aside, 1, 1).start()
+
+    @pl.when(inner)
+    def _():
+        line_copy(aside, 0, 2).start()
+
+    lax.fori_loop(HOLD, steps, pass_on, 0)
+
+    @pl.when(inner)
+    def _():
+        lax.fori_loop(LAG, MIDDLE, both, 0)
+        for way in range(3):
+            line_copy(mate, 0, way).wait_recv()
+        blocks = []
+        for held in [line] + [line_in.at[way] for way in range(3)]:
+            blocks += [held[c : c + 1, :].astype(jnp.float32) for c in range(spans)]
         rows = []
-        for l in range(spans):
-            row = jnp.zeros((1, local), jnp.float32)
-            for c in range(spans):
-                keep = (offset[c] == distance) & (place[c] == l)
-                row = row + decoded[c] * jnp.where(keep, 1.0, 0.0)
-            rows.append(row)
-        return jnp.concatenate(rows, 0)
-
-    for i, distance in enumerate(DISTANCES):
-        line[i] = placed(distance).astype(jnp.bfloat16)
-        line_copy(i).start()
-
-    @pl.when(inner)
-    def _():
-        lax.fori_loop(LAG, steps, both, 0)
-
-    total = placed(0)
-    for i in range(len(DISTANCES)):
-        line_copy(i).wait()
-        total = total + line_in[i].astype(jnp.float32)
-    moved_out[...] = total.astype(jnp.bfloat16)
+        for d in range(4 * spans):
+            total = blocks[0] * pick[0, d, 0:1, :].astype(jnp.float32)
+            for s in range(1, len(blocks)):
+                total = total + blocks[s] * pick[s, d, 0:1, :].astype(jnp.float32)
+            rows.append(total)
+        line_out[...] = jnp.concatenate(rows[2 * spans :], 0).astype(jnp.bfloat16)
+        line_cross_copy().start()
+        line_kept[...] = jnp.concatenate(rows[: 2 * spans], 0)
+        lax.fori_loop(MIDDLE, steps, both, 0)
+        line_cross_copy().wait_recv()
+        total = line_kept[...] + line_cross[...].astype(jnp.float32)
+        line_last[...] = total[spans:].astype(jnp.bfloat16)
+        line_final_copy().start()
+        moved_out[...] = total[:spans].astype(jnp.bfloat16)
 
     def land(k, _):
         final_copy(k).wait_recv()
@@ -559,7 +620,8 @@
 
     def inner_sent(k, _):
         raw_copy(aside, 0, 2, k).wait_send()
-        cross_copy(k).wait_send()
+        cross_copy(k, 0).wait_send()
+        cross_copy(k, 1).wait_send()
         final_copy(k).wait_send()
         return 0
 
@@ -567,6 +629,9 @@
     def _():
         lax.fori_loop(steps - LAG, steps, finish, 0)
         label_copy(aside, 0, 2).wait_send()
+        line_copy(aside, 0, 2).wait_send()
+        line_cross_copy().wait_send()
+        line_final_copy().wait_send()
         lax.fori_loop(0, steps, inner_sent, 0)
 
     @pl.when(outer)
@@ -574,6 +639,10 @@
         lax.fori_loop(0, steps, land, 0)
         label_copy(mate, 0, 0).wait_send()
         label_copy(mate_aside, 1, 1).wait_send()
+        line_copy(mate, 0, 0).wait_send()
+        line_copy(mate_aside, 1, 1).wait_send()
+        line_final_copy().wait_recv()
+        moved_out[...] = line_final[...]
         lax.fori_loop(0, steps, outer_sent, 0)
 
 
@@ -618,12 +687,12 @@
     parts = [pltpu.VMEM((8, width), f32), pltpu.VMEM((cores - 1, 8, width), f32)]
     steps = 2 * slots // ROWS
     if count == 2 * (REACH + 1):
-        function = relay_kernel
+        function, cache_spec = relay_kernel, away
 
         def blocks(*lead):
             return pltpu.VMEM(lead + (ROWS, local), bf16)
 
-        scratch = inputs + [
+        scratch = [pltpu.VMEM(self_cache.shape, bf16)] + inputs + [
             blocks(steps, spans),
             blocks(3, steps, spans),
             blocks(steps, 2 * spans),
@@ -634,20 +703,27 @@
             blocks(4 * spans, 4 * spans),
             pltpu.VMEM((8, 128), f32),
             pltpu.VMEM((3, 8, 128), f32),
-            pltpu.VMEM((moves, spans, local), bf16),
-            pltpu.VMEM((moves, spans, local), bf16),
+            pltpu.VMEM((spans, local), bf16),
+            pltpu.VMEM((3, spans, local), bf16),
+            pltpu.VMEM((2 * spans, local), f32),
+            pltpu.VMEM((2 * spans, local), bf16),
+            pltpu.VMEM((2 * spans, local), bf16),
+            pltpu.VMEM((spans, local), bf16),
+            pltpu.VMEM((spans, local), bf16),
             *parts,
-            dma((3,)),
+            dma((5,)),
             dma((2, steps)),
             dma((3, steps)),
-            dma((4, steps)),
+            dma((6, steps)),
             dma((2,)),
             dma((3,)),
-            dma((2, moves)),
+            dma((2,)),
+            dma((3,)),
+            dma((4,)),
             dma((2, cores - 1)),
         ]
     else:
-        function = kernel
+        function, cache_spec = kernel, vmem
         scratch = inputs + [
             pltpu.VMEM(self_cache.shape, bf16),
             parcels,
@@ -666,10 +742,10 @@
     return pl.pallas_call(
         functools.partial(function, count, cores),
         out_shape=(
-            jax.ShapeDtypeStruct(self_cache.shape, bf16),
-            jax.ShapeDtypeStruct((spans, local), bf16),
+            pltpu.VMEM(self_cache.shape, bf16),
+            pltpu.VMEM((spans, local), bf16),
         ),
-        in_specs=[smem] * 3 + [vmem] * 5 + [away] * 3,
+        in_specs=[smem] * 3 + [vmem] * 2 + [cache_spec] + [vmem] * 2 + [away] * 3,
         out_specs=(vmem, vmem),
         scratch_shapes=scratch,
         compiler_params=pltpu.CompilerParams(collective_id=0, has_side_effects=True),

time: 49.5 us -> 46.4 us (0.937)
  local copies, waits for them, and re-layouts: 3.23 us -> 1.42 us
  Pallas kernels: 45.5 us -> 44.2 us
    unnamed x2, local copies, waits for them, and re-layouts: 3.23 us -> 1.42 us
    pallas_call x1, Pallas kernels: 45.5 us -> 44.2 us  [body(): pl.pallas_call(functools.partial(function, count, cores), out_shape=(pltp...]
where the time goes in v4:
time: 46.4 us; the launch traced here: 46.2 us
  Pallas kernels  44.2 us (95%)
  local copies, waits for them, and re-layouts  1.42 us (3%)
  between operations  0.64 us (1%)
    pallas_call x1, Pallas kernels, body(): pl.pallas_call(functools.partial(function, count, cores), out_shape=(pltp...  44.2 us
    unnamed x2, local copies, waits for them, and re-layouts  1.42 us

profile of v4, /device:TPU:0, one launch (start us, length us, event | category | flops | bytes accessed | tf_op | source)
XLA Modules:
  0.0 46.2 jit_solution(11795795091397921693)
XLA Ops:
  0.6 44.2 %shard_map.122 = (bf16[2,2,128,640]{3,2,1,0:T(8,128)(2,1)S(1)}, bf16[2,640]{1,0:T(2,128)(2,1)S(1)}) custom-call(s32[2]{0:T(128)} %cache_len.1, s32[2]{0:T(128)} %finished.1, s32[2]{0:T(128)} %new_slot.1, bf16[2,1280]{1,0:T(2,128)(2,1)} %hidden.1, bf16[3,2,640]{2,1,0:T(2,128)(2,1)} %token_qkv.1, bf16[2,2,128,640]{3,2,1,0:T(8,128)(2,1)} %cache_hbm.1, ...), custom_call_target="tpu_custom_call" | custom-call | tf_op jit(solution)/shard_map/pallas_call | solution.py:742
  44.8 0.8 %copy.15 = bf16[2,2,128,640]{3,2,1,0:T(8,128)(2,1)} copy(bf16[2,2,128,640]{3,2,1,0:T(8,128)(2,1)S(1)} %get-tuple-element.2) | data formatting | bytes 1310720
  45.7 0.6 %copy.16 = bf16[2,640]{1,0:T(2,128)(2,1)} copy(bf16[2,640]{1,0:T(2,128)(2,1)S(1)} %get-tuple-element.3) | data formatting | bytes 5120

commit v5 on v4

--- a/solution.py
+++ b/solution.py
@@ -284,6 +284,7 @@
     kept,
     final_out,
     final_in,
+    final_far,
     pick,
     label,
     label_in,
@@ -328,7 +329,7 @@
     across = (REACH - level) * 2 + column
     beyond = (REACH - mate_level) * 2 + column
     others = [lax.rem(core + k, cores) for k in range(1, cores)]
-    for node in (mate, mate_aside):
+    for node in (mate, mate_aside, beyond):
         greet({"batch": node})
 
     @pl.when(inner)
@@ -368,14 +369,22 @@
     def raw_copy(node, lane, way, k):
         return to(node, own.at[k], raw_in.at[way, k], raw_send.at[lane, k], raw_recv.at[way, k])
 
-    def cross_copy(k, part):
-        first = (1 - part) * spans
+    def far_copy(k):
+        return to(
+            beyond,
+            cross_out.at[k, pl.ds(spans, spans)],
+            final_far.at[k],
+            hop_sems.at[0, k],
+            hop_sems.at[1, k],
+        )
+
+    def cross_copy(k):
         return to(
             across,
-            cross_out.at[k, pl.ds(first, spans)],
-            cross_in.at[k, pl.ds(first, spans)],
-            hop_sems.at[2 * part, k],
-            hop_sems.at[2 * part + 1, k],
+            cross_out.at[k, pl.ds(0, spans)],
+            cross_in.at[k],
+            hop_sems.at[2, k],
+            hop_sems.at[3, k],
         )
 
     def final_copy(k):
@@ -401,11 +410,11 @@
 
     @pl.when(inner)
     def _():
-        pl.semaphore_wait(barrier, 4 + len(others))
+        pl.semaphore_wait(barrier, 5 + len(others))
 
     @pl.when(outer)
     def _():
-        pl.semaphore_wait(barrier, 2 + len(others))
+        pl.semaphore_wait(barrier, 3 + len(others))
 
     position = lax.broadcasted_iota(jnp.int32, (rows_per, local), 0)
     ends = [cache_len[c] * alive[c] for c in range(spans)]
@@ -512,22 +521,23 @@
                 total = total + blocks[s] * pick[s, d]
             return total
 
-        for part in range(2):
-            for d in range((1 - part) * spans, (2 - part) * spans):
-                cross_out[k, d] = gathered(2 * spans + d)
-            cross_copy(k, part).start()
-        for d in range(2 * spans):
+        for d in range(spans, 2 * spans):
+            cross_out[k, d] = gathered(2 * spans + d)
+        far_copy(k).start()
+        for d in range(spans):
+            cross_out[k, d] = gathered(2 * spans + d)
+        cross_copy(k).start()
+        for d in range(spans):
+            final_out[k, d] = gathered(spans + d)
+        final_copy(k).start()
+        for d in range(spans):
             kept[k, d] = gathered(d)
         return 0
 
     def finish(k, _):
-        cross_copy(k, 0).wait_recv()
+        cross_copy(k).wait_recv()
         a, r = lax.div(k, per), lax.rem(k, per)
         start = pl.multiple_of(r * rows_per, rows_per)
-        for l in range(spans):
-            final_out[k, l] = kept[k, spans + l] + cross_in[k, spans + l]
-        final_copy(k).start()
-        cross_copy(k, 1).wait_recv()
         for l in range(spans):
             moved_cache[a, l, pl.ds(start, rows_per), :] = kept[k, l] + cross_in[k, l]
         return 0
@@ -607,10 +617,11 @@
 
     def land(k, _):
         final_copy(k).wait_recv()
+        far_copy(k).wait_recv()
         a, r = lax.div(k, per), lax.rem(k, per)
         start = pl.multiple_of(r * rows_per, rows_per)
         for l in range(spans):
-            moved_cache[a, l, pl.ds(start, rows_per), :] = final_in[k, l]
+            moved_cache[a, l, pl.ds(start, rows_per), :] = final_in[k, l] + final_far[k, l]
         return 0
 
     def outer_sent(k, _):
@@ -620,8 +631,8 @@
 
     def inner_sent(k, _):
         raw_copy(aside, 0, 2, k).wait_send()
-        cross_copy(k, 0).wait_send()
-        cross_copy(k, 1).wait_send()
+        far_copy(k).wait_send()
+        cross_copy(k).wait_send()
         final_copy(k).wait_send()
         return 0
 
@@ -696,8 +707,9 @@
             blocks(steps, spans),
             blocks(3, steps, spans),
             blocks(steps, 2 * spans),
-            blocks(steps, 2 * spans),
-            blocks(steps, 2 * spans),
+            blocks(steps, spans),
+            blocks(steps, spans),
+            blocks(steps, spans),
             blocks(steps, spans),
             blocks(steps, spans),
             blocks(4 * spans, 4 * spans),

time: 46.4 us -> 43.9 us (0.946)
  Pallas kernels: 44.2 us -> 41.7 us
    pallas_call x1, Pallas kernels: 44.2 us -> 41.7 us  [body(): pl.pallas_call(functools.partial(function, count, cores), out_shape=(pltp...]
where the time goes in v5:
time: 43.9 us; the launch traced here: 43.7 us
  Pallas kernels  41.7 us (95%)
  local copies, waits for them, and re-layouts  1.42 us (3%)
  between operations  0.64 us (1%)
    pallas_call x1, Pallas kernels, body(): pl.pallas_call(functools.partial(function, count, cores), out_shape=(pltp...  41.7 us
    unnamed x2, local copies, waits for them, and re-layouts  1.42 us

profile of v5, /device:TPU:0, one launch (start us, length us, event | category | flops | bytes accessed | tf_op | source)
XLA Modules:
  0.0 43.7 jit_solution(15875134585645718270)
XLA Ops:
  0.6 41.7 %shard_map.122 = (bf16[2,2,128,640]{3,2,1,0:T(8,128)(2,1)S(1)}, bf16[2,640]{1,0:T(2,128)(2,1)S(1)}) custom-call(s32[2]{0:T(128)} %cache_len.1, s32[2]{0:T(128)} %finished.1, s32[2]{0:T(128)} %new_slot.1, bf16[2,1280]{1,0:T(2,128)(2,1)} %hidden.1, bf16[3,2,640]{2,1,0:T(2,128)(2,1)} %token_qkv.1, bf16[2,2,128,640]{3,2,1,0:T(8,128)(2,1)} %cache_hbm.1, ...), custom_call_target="tpu_custom_call" | custom-call | tf_op jit(solution)/shard_map/pallas_call | solution.py:754
  42.3 0.8 %copy.15 = bf16[2,2,128,640]{3,2,1,0:T(8,128)(2,1)} copy(bf16[2,2,128,640]{3,2,1,0:T(8,128)(2,1)S(1)} %get-tuple-element.2) | data formatting | bytes 1310720
  43.1 0.6 %copy.16 = bf16[2,640]{1,0:T(2,128)(2,1)} copy(bf16[2,640]{1,0:T(2,128)(2,1)S(1)} %get-tuple-element.3) | data formatting | bytes 5120

commit v6 on v5

--- a/solution.py
+++ b/solution.py
@@ -260,19 +260,26 @@
 def relay_kernel(
     count,
     cores,
+    cache_len_hbm,
+    finished_hbm,
+    new_slot_hbm,
+    hidden_hbm,
+    token_qkv_hbm,
+    cache_hbm,
+    ln_gain_hbm,
+    ln_bias_hbm,
+    cross_hbm,
+    out_proj_hbm,
+    query_proj_hbm,
+    moved_cache,
+    moved_out,
     cache_len,
     finished,
     new_slot,
     hidden,
     token_qkv,
-    cache_hbm,
     ln_gain,
     ln_bias,
-    cross_hbm,
-    out_proj_hbm,
-    query_proj_hbm,
-    moved_cache,
-    moved_out,
     self_cache,
     cross,
     out_proj,
@@ -348,11 +355,20 @@
                 (cross_hbm, cross),
                 (cache_hbm.at[0], self_cache.at[0]),
                 (cache_hbm.at[1], self_cache.at[1]),
+                (cache_len_hbm, cache_len),
+                (finished_hbm, finished),
+                (new_slot_hbm, new_slot),
+                (hidden_hbm, hidden),
+                (token_qkv_hbm, token_qkv),
+                (ln_gain_hbm, ln_gain),
+                (ln_bias_hbm, ln_bias),
             ]
         )
     ]
-    for i in (3, 4, 0, 1, 2):
+    for i in [3, *range(5, len(loads)), 4, 0, 1, 2]:
         loads[i].start()
+    for load in loads[5:]:
+        load.wait()
 
     alive = [jnp.where(finished[c] == 0, 1, 0) for c in range(spans)]
 
@@ -698,12 +714,18 @@
     parts = [pltpu.VMEM((8, width), f32), pltpu.VMEM((cores - 1, 8, width), f32)]
     steps = 2 * slots // ROWS
     if count == 2 * (REACH + 1):
-        function, cache_spec = relay_kernel, away
+        function, specs = relay_kernel, [away] * 8
 
         def blocks(*lead):
             return pltpu.VMEM(lead + (ROWS, local), bf16)
 
-        scratch = [pltpu.VMEM(self_cache.shape, bf16)] + inputs + [
+        small = [pltpu.SMEM((spans,), jnp.int32)] * 3 + [
+            pltpu.VMEM(hidden.shape, bf16),
+            pltpu.VMEM(token_qkv.shape, bf16),
+            pltpu.VMEM(ln_gain.shape, f32),
+            pltpu.VMEM(ln_bias.shape, f32),
+        ]
+        scratch = small + [pltpu.VMEM(self_cache.shape, bf16)] + inputs + [
             blocks(steps, spans),
             blocks(3, steps, spans),
             blocks(steps, 2 * spans),
@@ -723,7 +745,7 @@
             pltpu.VMEM((spans, local), bf16),
             pltpu.VMEM((spans, local), bf16),
             *parts,
-            dma((5,)),
+            dma((12,)),
             dma((2, steps)),
             dma((3, steps)),
             dma((6, steps)),
@@ -735,7 +757,7 @@
             dma((2, cores - 1)),
         ]
     else:
-        function, cache_spec = kernel, vmem
+        function, specs = kernel, [smem] * 3 + [vmem] * 5
         scratch = inputs + [
             pltpu.VMEM(self_cache.shape, bf16),
             parcels,
@@ -757,7 +779,7 @@
             pltpu.VMEM(self_cache.shape, bf16),
             pltpu.VMEM((spans, local), bf16),
         ),
-        in_specs=[smem] * 3 + [vmem] * 2 + [cache_spec] + [vmem] * 2 + [away] * 3,
+        in_specs=specs + [away] * 3,
         out_specs=(vmem, vmem),
         scratch_shapes=scratch,
         compiler_params=pltpu.CompilerParams(collective_id=0, has_side_effects=True),

time: 43.9 us -> 43.1 us (0.982)
  Pallas kernels: 41.7 us -> 40.9 us
    pallas_call x1, Pallas kernels: 41.7 us -> 40.9 us  [body(): pl.pallas_call(functools.partial(function, count, cores), out_shape=(pltp...]
where the time goes in v6:
time: 43.1 us; the launch traced here: 43 us
  Pallas kernels  40.9 us (95%)
  local copies, waits for them, and re-layouts  1.42 us (3%)
  between operations  0.64 us (1%)
    pallas_call x1, Pallas kernels, body(): pl.pallas_call(functools.partial(function, count, cores), out_shape=(pltp...  40.9 us
    unnamed x2, local copies, waits for them, and re-layouts  1.42 us

profile of v6, /device:TPU:0, one launch (start us, length us, event | category | flops | bytes accessed | tf_op | source)
XLA Modules:
  0.0 43.0 jit_solution(14119705166254605033)
XLA Ops:
  0.6 40.9 %shard_map.122 = (bf16[2,2,128,640]{3,2,1,0:T(8,128)(2,1)S(1)}, bf16[2,640]{1,0:T(2,128)(2,1)S(1)}) custom-call(s32[2]{0:T(128)} %cache_len_hbm.1, s32[2]{0:T(128)} %finished_hbm.1, s32[2]{0:T(128)} %new_slot_hbm.1, bf16[2,1280]{1,0:T(2,128)(2,1)} %hidden_hbm.1, bf16[3,2,640]{2,1,0:T(2,128)(2,1)} %token_qkv_hbm.1, bf16[2,2,128,640]{3,2,1,0:T(8,128)(2,1)} %cache_hbm.1, ...), custom_call_target="tpu_custom_call" | custom-call | tf_op jit(solution)/shard_map/pallas_call | solution.py:776
  41.6 0.8 %copy.15 = bf16[2,2,128,640]{3,2,1,0:T(8,128)(2,1)} copy(bf16[2,2,128,640]{3,2,1,0:T(8,128)(2,1)S(1)} %get-tuple-element.2) | data formatting | bytes 1310720
  42.4 0.6 %copy.16 = bf16[2,640]{1,0:T(2,128)(2,1)} copy(bf16[2,640]{1,0:T(2,128)(2,1)S(1)} %get-tuple-element.3) | data formatting | bytes 5120
